TPU v7x, 8 devices: a whole 2x2x1 slice. The times are simulated.
8 devices in a mesh: fsdp: 8 (over z, y, x, core).
Axes of the slice: x: 2, y: 2, z: 1, core: 2. Of those that a mesh axis runs over, the one named last changes fastest.
Arguments:
- hidden: bfloat16 [48, 512, 1536], P('fsdp')
- grad_out: bfloat16 [48, 512, 1536], P('fsdp')
- positions: int32 [48, 512], P('fsdp')
- norm1_gain: bfloat16 [1536], P('fsdp')
- norm2_gain: bfloat16 [1536], P('fsdp')
- q_norm_gain: bfloat16 [128], replicated
- k_norm_gain: bfloat16 [128], replicated
- w_q: bfloat16 [1536, 1536], P('fsdp')
- w_k: bfloat16 [1536, 256], P('fsdp')
- w_v: bfloat16 [1536, 256], P('fsdp')
- w_o: bfloat16 [1536, 1536], P('fsdp')
- w_gate: bfloat16 [1536, 8960], P('fsdp')
- w_up: bfloat16 [1536, 8960], P('fsdp')
- w_down: bfloat16 [8960, 1536], P('fsdp')
Outputs:
- output 1: bfloat16 [48, 512, 1536], P('fsdp')
- output 2: bfloat16 [48, 512, 1536], P('fsdp')
- output 3: float32 [1536], P('fsdp')
- output 4: float32 [1536], P('fsdp')
- output 5: float32 [128], replicated
- output 6: float32 [128], replicated
- output 7: float32 [1536, 1536], P('fsdp')
- output 8: float32 [1536, 256], P('fsdp')
- output 9: float32 [1536, 256], P('fsdp')
- output 10: float32 [1536, 1536], P('fsdp')
- output 11: float32 [1536, 8960], P('fsdp')
- output 12: float32 [1536, 8960], P('fsdp')
- output 13: float32 [8960, 1536], P('fsdp')
All inputs are finite; a program needn't handle non-finite values.
Results may differ from a plain program's by a relative error of at most 0.02.
Values are sent between devices in bfloat16 or wider.
A program may use at most 1 GiB of HBM per device.

v0:
```python
import jax
import jax.numpy as jnp
from jax import lax
from jax.sharding import PartitionSpec as P

RMS_EPS = 1e-6
ROPE_THETA = 1000000.0


def rms_scale(tensor):
    return lax.rsqrt(jnp.mean(tensor * tensor, axis=-1, keepdims=True) + RMS_EPS)


def norm_backward(d_unit, unit_val, scale_val):
    return scale_val * (d_unit - unit_val * jnp.mean(d_unit * unit_val, axis=-1, keepdims=True))


def rotate_half(tensor):
    half_dim = tensor.shape[-1] // 2
    return jnp.concatenate([-tensor[..., half_dim:], tensor[..., :half_dim]], axis=-1)


def matmul(left_op, right_op):
    return jnp.dot(left_op, right_op, preferred_element_type=jnp.float32)


def matmul_tn(left_op, right_op):
    return lax.dot_general(left_op, right_op, (((0,), (0,)), ((), ())), preferred_element_type=jnp.float32)


def matmul_nt(left_op, right_op):
    return lax.dot_general(left_op, right_op, (((1,), (1,)), ((), ())), preferred_element_type=jnp.float32)


def rope_tables(positions, head_dim):
    inv_freq = ROPE_THETA ** (-2.0 * jnp.arange(head_dim // 2, dtype=jnp.float32) / head_dim)
    rope_angle = positions.reshape(-1, 1).astype(jnp.float32) * inv_freq
    cos_half = jnp.cos(rope_angle)
    sin_half = jnp.sin(rope_angle)
    cos_t = jnp.concatenate([cos_half, cos_half], axis=-1)[:, None, :]
    sin_t = jnp.concatenate([sin_half, sin_half], axis=-1)[:, None, :]
    return cos_t, sin_t


def head_norm_rope(projected, num_heads, head_dim, gain_vec, cos_t, sin_t):
    heads_float = projected.reshape(projected.shape[0], num_heads, head_dim).astype(jnp.float32)
    head_scale = rms_scale(heads_float)
    head_unit = heads_float * head_scale
    scaled = head_unit * gain_vec.astype(jnp.float32)
    rotated = (scaled * cos_t + rotate_half(scaled) * sin_t).astype(jnp.bfloat16)
    return rotated, head_unit, head_scale


def head_norm_rope_backward(d_rotated, head_unit, head_scale, gain_vec, cos_t, sin_t):
    d_scaled = d_rotated * cos_t - rotate_half(d_rotated * sin_t)
    d_gain = jnp.sum(d_scaled * head_unit, axis=(0, 1))
    d_projected = norm_backward(d_scaled * gain_vec.astype(jnp.float32), head_unit, head_scale)
    return d_projected.reshape(d_projected.shape[0], -1).astype(jnp.bfloat16), d_gain


def forward_local(hidden, positions, weights):
    norm1_gain, norm2_gain, q_norm_gain, k_norm_gain, w_q, w_k, w_v, w_o, w_gate, w_up, w_down = weights
    batch_local, seq_len, model_width = hidden.shape
    head_dim = q_norm_gain.shape[0]
    num_heads = w_q.shape[1] // head_dim
    kv_heads = w_k.shape[1] // head_dim
    tokens = batch_local * seq_len
    x_float = hidden.reshape(tokens, model_width).astype(jnp.float32)
    x_scale = rms_scale(x_float)
    x_unit = x_float * x_scale
    normed = (x_unit * norm1_gain.astype(jnp.float32)).astype(jnp.bfloat16)
    q_proj = matmul(normed, w_q).astype(jnp.bfloat16)
    k_proj = matmul(normed, w_k).astype(jnp.bfloat16)
    v_proj = matmul(normed, w_v).astype(jnp.bfloat16)
    cos_t, sin_t = rope_tables(positions, head_dim)
    q_rot, q_unit, q_scale = head_norm_rope(q_proj, num_heads, head_dim, q_norm_gain, cos_t, sin_t)
    k_rot, k_unit, k_scale = head_norm_rope(k_proj, kv_heads, head_dim, k_norm_gain, cos_t, sin_t)
    q_grouped = q_rot.reshape(batch_local, seq_len, kv_heads, num_heads // kv_heads, head_dim)
    k_seq = k_rot.reshape(batch_local, seq_len, kv_heads, head_dim)
    v_seq = v_proj.reshape(batch_local, seq_len, kv_heads, head_dim)
    scores = jnp.einsum("bskgd,btkd->bksgt", q_grouped, k_seq, preferred_element_type=jnp.float32) * (head_dim ** -0.5)
    causal = (jnp.arange(seq_len)[:, None] >= jnp.arange(seq_len)[None, :])[:, None, :]
    attn_probs = jax.nn.softmax(jnp.where(causal, scores, -1e30), axis=-1)
    attn_ctx = jnp.einsum("bksgt,btkd->bskgd", attn_probs.astype(jnp.bfloat16), v_seq, preferred_element_type=jnp.float32).astype(jnp.bfloat16).reshape(tokens, num_heads * head_dim)
    attn_out = matmul(attn_ctx, w_o).astype(jnp.bfloat16)
    resid_float = (x_float + attn_out.astype(jnp.float32)).astype(jnp.bfloat16).astype(jnp.float32)
    r_scale = rms_scale(resid_float)
    r_unit = resid_float * r_scale
    mlp_in = (r_unit * norm2_gain.astype(jnp.float32)).astype(jnp.bfloat16)
    gate_proj = matmul(mlp_in, w_gate).astype(jnp.bfloat16)
    up_proj = matmul(mlp_in, w_up).astype(jnp.bfloat16)
    mlp_act = (jax.nn.silu(gate_proj.astype(jnp.float32)) * up_proj.astype(jnp.float32)).astype(jnp.bfloat16)
    down_proj = matmul(mlp_act, w_down).astype(jnp.bfloat16)
    layer_out = (resid_float + down_proj.astype(jnp.float32)).astype(jnp.bfloat16).reshape(batch_local, seq_len, model_width)
    saved_acts = {"x_unit": x_unit, "x_scale": x_scale, "normed": normed, "cos_t": cos_t, "sin_t": sin_t, "q_unit": q_unit, "q_scale": q_scale, "k_unit": k_unit, "k_scale": k_scale, "q_grouped": q_grouped, "k_seq": k_seq, "v_seq": v_seq, "attn_probs": attn_probs, "attn_ctx": attn_ctx, "r_unit": r_unit, "r_scale": r_scale, "mlp_in": mlp_in, "gate_proj": gate_proj, "up_proj": up_proj, "mlp_act": mlp_act}
    return layer_out, saved_acts


def backward_local(grad_out, saved_acts, weights):
    norm1_gain, norm2_gain, q_norm_gain, k_norm_gain, w_q, w_k, w_v, w_o, w_gate, w_up, w_down = weights
    batch_local, seq_len, model_width = grad_out.shape
    tokens = batch_local * seq_len
    q_grouped = saved_acts["q_grouped"]
    kv_heads = q_grouped.shape[2]
    kv_group = q_grouped.shape[3]
    head_dim = q_grouped.shape[4]
    num_heads = kv_heads * kv_group
    dy_flat = grad_out.reshape(tokens, model_width)
    grad_down = matmul_tn(saved_acts["mlp_act"], dy_flat)
    d_mlp_act = matmul_nt(dy_flat, w_down)
    gate_float = saved_acts["gate_proj"].astype(jnp.float32)
    gate_sig = jax.nn.sigmoid(gate_float)
    d_up_proj = (d_mlp_act * gate_float * gate_sig).astype(jnp.bfloat16)
    d_gate_proj = (d_mlp_act * saved_acts["up_proj"].astype(jnp.float32) * gate_sig * (1.0 + gate_float * (1.0 - gate_sig))).astype(jnp.bfloat16)
    grad_gate = matmul_tn(saved_acts["mlp_in"], d_gate_proj)
    grad_up = matmul_tn(saved_acts["mlp_in"], d_up_proj)
    d_mlp_in = matmul_nt(d_gate_proj, w_gate) + matmul_nt(d_up_proj, w_up)
    grad_norm2 = jnp.sum(d_mlp_in * saved_acts["r_unit"], axis=0)
    d_resid = dy_flat.astype(jnp.float32) + norm_backward(d_mlp_in * norm2_gain.astype(jnp.float32), saved_acts["r_unit"], saved_acts["r_scale"])
    d_resid_bf = d_resid.astype(jnp.bfloat16)
    grad_wo = matmul_tn(saved_acts["attn_ctx"], d_resid_bf)
    d_attn_ctx = matmul_nt(d_resid_bf, w_o).astype(jnp.bfloat16).reshape(batch_local, seq_len, kv_heads, kv_group, head_dim)
    attn_probs = saved_acts["attn_probs"]
    d_value = jnp.einsum("bksgt,bskgd->btkd", attn_probs.astype(jnp.bfloat16), d_attn_ctx, preferred_element_type=jnp.float32).astype(jnp.bfloat16).reshape(tokens, kv_heads * head_dim)
    d_probs = jnp.einsum("bskgd,btkd->bksgt", d_attn_ctx, saved_acts["v_seq"], preferred_element_type=jnp.float32)
    d_scores = attn_probs * (d_probs - jnp.sum(attn_probs * d_probs, axis=-1, keepdims=True))
    d_scores = (d_scores * (head_dim ** -0.5)).astype(jnp.bfloat16)
    d_q_rot = jnp.einsum("bksgt,btkd->bskgd", d_scores, saved_acts["k_seq"], preferred_element_type=jnp.float32).reshape(tokens, num_heads, head_dim)
    d_k_rot = jnp.einsum("bksgt,bskgd->btkd", d_scores, q_grouped, preferred_element_type=jnp.float32).reshape(tokens, kv_heads, head_dim)
    d_query, grad_qgain = head_norm_rope_backward(d_q_rot, saved_acts["q_unit"], saved_acts["q_scale"], q_norm_gain, saved_acts["cos_t"], saved_acts["sin_t"])
    d_key, grad_kgain = head_norm_rope_backward(d_k_rot, saved_acts["k_unit"], saved_acts["k_scale"], k_norm_gain, saved_acts["cos_t"], saved_acts["sin_t"])
    normed = saved_acts["normed"]
    grad_wq = matmul_tn(normed, d_query)
    grad_wk = matmul_tn(normed, d_key)
    grad_wv = matmul_tn(normed, d_value)
    d_normed = matmul_nt(d_query, w_q) + matmul_nt(d_key, w_k) + matmul_nt(d_value, w_v)
    grad_norm1 = jnp.sum(d_normed * saved_acts["x_unit"], axis=0)
    d_hidden = (d_resid + norm_backward(d_normed * norm1_gain.astype(jnp.float32), saved_acts["x_unit"], saved_acts["x_scale"])).astype(jnp.bfloat16)
    local_grads = (grad_norm1, grad_norm2, grad_qgain, grad_kgain, grad_wq, grad_wk, grad_wv, grad_wo, grad_gate, grad_up, grad_down)
    return d_hidden.reshape(batch_local, seq_len, model_width), local_grads


def solution(mesh):
    axis_name = mesh.axis_names[0]
    group_size = mesh.shape[axis_name]
    sharded = P(axis_name)
    in_specs = (sharded, sharded, sharded, sharded, sharded, P(), P()) + (sharded,) * 7
    out_specs = (sharded, sharded, sharded, sharded, P(), P()) + (sharded,) * 7

    def gather_weights(row_shards, q_norm_gain, k_norm_gain):
        full_rows = tuple(lax.all_gather(row_shard, axis_name, axis=0, tiled=True) for row_shard in row_shards)
        return (full_rows[0], full_rows[1], q_norm_gain, k_norm_gain) + full_rows[2:]

    def device_step(hidden, grad_out, positions, norm1_gain, norm2_gain, q_norm_gain, k_norm_gain, w_q, w_k, w_v, w_o, w_gate, w_up, w_down):
        row_shards = (norm1_gain, norm2_gain, w_q, w_k, w_v, w_o, w_gate, w_up, w_down)
        weights_fwd = gather_weights(row_shards, q_norm_gain, k_norm_gain)
        layer_out, saved_acts = forward_local(hidden, positions, weights_fwd)
        layer_out, row_shards = lax.optimization_barrier((layer_out, row_shards))
        weights_bwd = gather_weights(row_shards, q_norm_gain, k_norm_gain)
        d_hidden, local_grads = backward_local(grad_out, saved_acts, weights_bwd)
        inv_tokens = 1.0 / (hidden.shape[0] * hidden.shape[1] * group_size)
        row_grads = local_grads[:2] + local_grads[4:]
        reduced = tuple(lax.psum_scatter(row_grad * inv_tokens, axis_name, scatter_dimension=0, tiled=True) for row_grad in row_grads)
        qgain_sum = lax.psum(local_grads[2] * inv_tokens, axis_name)
        kgain_sum = lax.psum(local_grads[3] * inv_tokens, axis_name)
        return (layer_out, d_hidden, reduced[0], reduced[1], qgain_sum, kgain_sum) + reduced[2:]

    return jax.shard_map(device_step, mesh=mesh, in_specs=in_specs, out_specs=out_specs, check_vma=False)
```

profile of v0, /device:TPU:0, one launch (start us, length us, event | category | flops | bytes accessed | tf_op | source)
XLA Modules:
  0.0 2949.9 jit_solution(11962509640952207922)
XLA Ops:
  13.1 25.8 all-reduce.8
  44.6 18.3 all_gather.57
  63.0 9.6 fusion.47
  83.9 29.7 %all_gather.55 = bf16[1536,256]{1,0:T(8,128)(2,1)S(1)} all-gather(bf16[192,256]{1,0:T(8,128)(2,1)S(1)} %copy-done.26), channel_id=1, replica_groups=mesh['fsdp'=8] {'fsdp'}, dimensions={0}, use_global_device_ids=true | all-gather | bytes 884736 | tf_op jit(solution)/shard_map/all_gather | solution.py:151
  113.6 7.5 convolution_convert_fusion.7
  138.3 21.2 fusion.62
  159.5 25.4 reshape.310
  184.9 8.9 multiply_reduce_fusion.3
  194.0 8.3 multiply_multiply_fusion
  209.6 12.9 concatenate.55
  222.6 14.7 copy.85
  237.3 13.4 concatenate.56
  250.8 10.0 copy.86
  261.6 22.7 fusion.41
  284.3 34.5 %fusion.106 = (f32[6,2,512,6]{2,3,1,0:T(8,128)S(1)}, f32[6,2,512,6,512]{2,4,3,1,0:T(8,128)}) fusion(pred[512,512]{0,1:T(8,128)(4,1)S(1)} %copy-done.28, bf16[6,512,2,6,128]{1,4,3,2,0:T(8,128)(2,1)} %fusion.41, bf16[6,512,2,128,1]{1,3,4,2,0:T(8,128)(2,1)} %fusion.84), kind=kOutput, calls=%fused_computation.178 | convolution fusion | flops 4907336192 | bytes 86917120 | tf_op jit(solution)/shard_map/sub | solution.py:83
  318.7 29.0 convert_bitcast_fusion
  347.8 16.3 copy.95
  364.1 19.9 reshape.281
  384.0 23.7 fusion.35
  407.8 98.7 %convolution_convert_fusion.1 = bf16[3072,8960]{1,0:T(8,128)(2,1)} fusion(bf16[1536,8960]{1,0:T(8,128)(2,1)} %all-gather.15.cloned.1.call-done, bf16[3072,1536]{1,0:T(8,128)(2,1)} %get-tuple-element.68, f32[1536]{0:T(1024)S(1)} %copy-done.46, f32[3072]{0:T(1024)S(1)} %add_rsqrt_fusion.3), kind=kOutput, calls=%fused_computation.25 | convolution fusion | flops 84603568128 | bytes 92030976 | tf_op jit(solution)/shard_map/dot_general | solution.py:24
  506.5 126.4 %fusion.2 = (bf16[3072,8960]{1,0:T(8,128)(2,1)}, bf16[3072,8960]{1,0:T(8,128)(2,1)}) fusion(bf16[3072,8960]{1,0:T(8,128)(2,1)} %convolution_convert_fusion.1, bf16[1536,8960]{1,0:T(8,128)(2,1)} %all-gather.17.cloned.1.call-done, bf16[3072,1536]{1,0:T(8,128)(2,1)} %get-tuple-element.68, f32[1536]{0:T(1024)S(1)} %copy-done.46, f32[3072]{0:T(1024)S(1)} %add_rsqrt_fusion.3), kind=kOutput, calls=%fused_computation.8 | convolution fusion | flops 84823769088 | bytes 202131456 | tf_op jit(solution)/shard_map/dot_general | solution.py:24
  632.9 98.7 %fusion.36 = bf16[3072,1536]{1,0:T(8,128)(2,1)} fusion(bf16[3072,1536]{1,0:T(8,128)(2,1)} %get-tuple-element.68, bf16[3072,8960]{1,0:T(8,128)(2,1)} %get-tuple-element.69, bf16[8960,1536]{1,0:T(8,128)(2,1)} %all-gather.19.cloned.1.call-done), kind=kOutput, calls=%fused_computation.51 | convolution fusion | flops 84580761600 | bytes 101449728 | tf_op jit(solution)/shard_map/dot_general | solution.py:24
  744.7 9.5 fusion.56
  754.7 24.0 all-reduce.7
  779.7 83.6 %all-gather.21.cloned.1.call-done = bf16[8960,1536]{1,0:T(8,128)(2,1)} async-done(((bf16[1120,1536]{1,0:T(8,128)(2,1)}), bf16[8960,1536]{1,0:T(8,128)(2,1)}) %all-gather.21.cloned.1.call-update) | async-done | bytes 27525136 | tf_op jit(solution)/shard_map/all_gather | solution.py:151
  863.3 153.9 %fusion.11 = (bf16[3072,8960]{1,0:T(8,128)(2,1)}, bf16[3072,8960]{1,0:T(8,128)(2,1)}) fusion(bf16[3072,8960]{1,0:T(8,128)(2,1)} %convolution_convert_fusion.1, bf16[3072,8960]{1,0:T(8,128)(2,1)} %get-tuple-element.70, bf16[8960,1536]{1,0:T(8,128)(2,1)} %all-gather.21.cloned.1.call-done, bf16[3072,1536]{1,0:T(8,128)(2,1)} %bitcast.221), kind=kOutput, calls=%fused_computation.17 | convolution fusion | flops 84970045440 | bytes 257163264 | tf_op jit(solution)/shard_map/dot_general | solution.py:32
  1017.3 96.1 %fusion.107 = f32[3072,1536]{1,0:T(8,128)} fusion(bf16[3072,8960]{1,0:T(8,128)(2,1)} %get-tuple-element.50, bf16[1536,8960]{1,0:T(8,128)(2,1)} %all-gather.23.cloned.1.call-done), kind=kOutput, calls=%fused_computation.179 | convolution fusion | flops 84557168640 | bytes 101449728 | tf_op jit(solution)/shard_map/dot_general | solution.py:32
  1113.4 12.8 all-gather.25.cloned.1.call-done
  1126.3 104.8 %fusion.34 = (f32[1536]{0:T(1024)}, f32[3072]{0:T(1024)S(1)}, f32[3072,1536]{1,0:T(8,128)}) fusion(bf16[3072,1536]{1,0:T(8,128)(2,1)} %get-tuple-element.68, f32[3072]{0:T(1024)S(1)} %copy-done.38, f32[1536]{0:T(1024)S(1)} %copy-done.41, f32[3072,1536]{1,0:T(8,128)} %fusion.107, bf16[3072,8960]{1,0:T(8,128)(2,1)} %get-tuple-element.49, ...), kind=kOutput, calls=%fused_computation.49 | convolution fusion | flops 84594917376 | bytes 129798144 | tf_op jit(solution)/shard_map/dot_general | solution.py:32
  1231.0 20.8 fusion.33
  1251.8 21.1 convolution_convert_fusion.2
  1272.8 19.9 reshape.284
  1292.7 15.3 copy.120
  1308.1 29.8 %fusion.94 = f32[6,2,512,6,512]{2,4,3,1,0:T(8,128)} fusion(bf16[6,512,2,6,128]{1,4,3,2,0:T(8,128)(2,1)} %copy.120, bf16[6,512,2,128,1]{3,2,1,0,4:T(2,128)(2,1)S(1)} %bitcast.229), kind=kOutput, calls=%fused_computation.152 | convolution fusion | flops 4831838208 | bytes 86507520 | tf_op jit(solution)/shard_map/bskgd,btkd->bksgt/dot_general | solution.py:125
  1337.9 97.3 %fusion.63 = f32[6,512,2,6,128]{1,4,3,2,0:T(8,128)} fusion(bf16[6,512,2,128,1]{1,3,4,2,0:T(8,128)(2,1)S(1)} %copy-done.21, f32[6,2,512,6,512]{2,4,3,1,0:T(8,128)} %fusion.94, f32[6,2,512,6,512]{2,4,3,1,0:T(8,128)} %get-tuple-element.66, f32[6,2,512,6]{2,3,1,0:T(8,128)S(1)} %copy-done.63), kind=kOutput, calls=%fused_computation.104 | convolution fusion | flops 4963996160 | bytes 171589632 | tf_op jit(solution)/shard_map/bksgt,btkd->bskgd/dot_general | solution.py:128
  1435.2 111.3 %fusion.81 = f32[6,512,2,128]{1,3,2,0:T(8,128)S(1)} fusion(bf16[6,512,2,6,128]{1,4,3,2,0:T(8,128)(2,1)} %fusion.41, f32[6,2,512,6,512]{2,4,3,1,0:T(8,128)} %fusion.94, f32[6,2,512,6,512]{2,4,3,1,0:T(8,128)} %get-tuple-element.66, f32[6,2,512,6]{2,3,1,0:T(8,128)S(1)} %copy-done.63), kind=kOutput, calls=%fused_computation.136 | convolution fusion | flops 4963996160 | bytes 163725312 | tf_op jit(solution)/shard_map/bksgt,bskgd->btkd/dot_general | solution.py:129
  1553.0 18.6 copy.103
  1579.0 13.3 slice_negate_fusion
  1592.3 15.0 copy.107
  1607.3 15.1 copy.108
  1640.6 7.6 multiply_reduce_fusion.4
  1662.3 7.6 convolution_multiply_fusion.6
  1669.8 29.2 fusion.88
  1699.2 26.8 multiply_reduce_fusion.1
  1726.0 22.1 copy.145
  1748.5 16.6 pad_maximum_fusion
  1765.1 18.7 copy.104
  1783.7 23.7 copy.159
  1811.4 8.1 convolution_multiply_fusion.5
  1819.6 20.0 fusion.39
  1843.2 19.0 convolution_multiply_fusion.4
  1862.4 24.2 convolution_multiply_fusion.3
  1886.7 97.1 %convolution_multiply_fusion = f32[8960,1536]{1,0:T(8,128)} fusion(bf16[3072,8960]{1,0:T(8,128)(2,1)} %get-tuple-element.69, bf16[3072,1536]{1,0:T(8,128)(2,1)} %bitcast.222), kind=kOutput, calls=%fused_computation.26 | convolution fusion | flops 84570931200 | bytes 119537664 | tf_op jit(solution)/shard_map/dot_general | solution.py:28
  1984.5 100.3 %convolution_multiply_fusion.1 = f32[1536,8960]{1,0:T(8,128)} fusion(bf16[3072,8960]{1,0:T(8,128)(2,1)} %get-tuple-element.49, bf16[3072,1536]{1,0:T(8,128)(2,1)} %get-tuple-element.68, f32[1536]{0:T(1024)S(1)} %copy-done.47, f32[3072]{0:T(1024)S(1)} %copy-done.39), kind=kOutput, calls=%fused_computation.27 | convolution fusion | flops 84589805568 | bytes 119556096 | tf_op jit(solution)/shard_map/dot_general | solution.py:28
  2084.9 100.3 %convolution_multiply_fusion.2 = f32[1536,8960]{1,0:T(8,128)} fusion(bf16[3072,8960]{1,0:T(8,128)(2,1)} %get-tuple-element.50, bf16[3072,1536]{1,0:T(8,128)(2,1)} %get-tuple-element.68, f32[1536]{0:T(1024)S(1)} %copy-done.47, f32[3072]{0:T(1024)S(1)} %copy-done.39), kind=kOutput, calls=%fused_computation.28 | convolution fusion | flops 84589805568 | bytes 119556096 | tf_op jit(solution)/shard_map/dot_general | solution.py:28
  2186.1 19.8 all_gather.69
  2205.9 19.2 all_gather.70
  2225.1 8.1 fusion.108
  2233.2 8.0 fusion.86
  2241.2 38.2 %fusion.53 = (f32[1536]{0:T(1024)S(1)}, f32[3072]{0:T(1024)S(1)}, f32[3072,1536]{1,0:T(8,128)}) fusion(bf16[6,512,1536]{2,1,0:T(8,128)(2,1)} %param.14, f32[3072]{0:T(1024)S(1)} %copy-done.34, f32[1536]{0:T(1024)S(1)} %convert_element_type.237, f32[3072,1536]{1,0:T(8,128)} %fusion.86, f32[3072,1536]{1,0:T(8,128)} %fusion.108, ...), kind=kOutput, calls=%fused_computation.79 | convolution fusion | flops 14537976832 | bytes 80252928 | tf_op jit(solution)/shard_map/dot_general | solution.py:32
  2279.5 23.9 all-reduce.6
  2304.7 20.2 fusion.52
  2325.0 308.7 %reduce-scatter.18.cloned.1.call-done = f32[192,8960]{1,0:T(8,128)} async-done(((f32[1536,8960]{1,0:T(8,128)}), f32[192,8960]{1,0:T(8,128)}) %reduce-scatter.18.cloned.1.call-update) | async-done | bytes 6881296 | tf_op jit(solution)/shard_map/reduce_scatter | solution.py:163
  2633.6 309.5 %reduce-scatter.16.cloned.1.call-done = f32[192,8960]{1,0:T(8,128)} async-done(((f32[1536,8960]{1,0:T(8,128)}), f32[192,8960]{1,0:T(8,128)}) %reduce-scatter.16.cloned.1.call-update) | async-done | bytes 6881296 | tf_op jit(solution)/shard_map/reduce_scatter | solution.py:163
  (253 shorter events, 119.7 us)
Async XLA Ops:
  7.2 37.4 %copy-start.24 = (bf16[192,256]{1,0:T(8,128)(2,1)S(1)}, bf16[192,256]{1,0:T(8,128)(2,1)}, u32[]{:S(2)}) copy-start(bf16[192,256]{1,0:T(8,128)(2,1)} %param.22) | copy-start | bytes 294916
  7.2 131.1 %all-gather.11.cloned.1.call-start = ((), (), s32[]{:S(2)}) async-start(), calls=%async_computation.7 | async-start | bytes 5308416 | tf_op jit(solution)/shard_map/all_gather | solution.py:151
  7.9 376.1 %all-gather.13.cloned.1.call-start = ((), (), s32[]{:S(2)}) async-start(), calls=%async_computation.8 | async-start | bytes 5308416 | tf_op jit(solution)/shard_map/all_gather | solution.py:151
  8.7 399.1 %all-gather.15.cloned.1.call-start = ((), (), s32[]{:S(2)}) async-start(), calls=%async_computation.9 | async-start | bytes 30965760 | tf_op jit(solution)/shard_map/all_gather | solution.py:151
  9.4 497.1 %all-gather.17.cloned.1.call-start = ((), (), s32[]{:S(2)}) async-start(), calls=%async_computation.10 | async-start | bytes 30965760 | tf_op jit(solution)/shard_map/all_gather | solution.py:151
  10.0 622.9 %all-gather.19.cloned.1.call-start = ((), (), s32[]{:S(2)}) async-start(), calls=%async_computation.11 | async-start | bytes 30965760 | tf_op jit(solution)/shard_map/all_gather | solution.py:151
  10.6 852.8 %all-gather.21.cloned.1.call-start = ((), (), s32[]{:S(2)}) async-start(), calls=%async_computation.12 | async-start | bytes 30965760 | tf_op jit(solution)/shard_map/all_gather | solution.py:151
  10.6 116.8 %copy-start.53 = (f32[64]{0:T(128)}, f32[64]{0:T(128)S(1)}, u32[]{:S(2)}) copy-start(f32[64]{0:T(128)S(1)} %multiply_power_fusion) | copy-start | bytes 772
  38.9 24.1 copy-start.35
  44.6 18.4 copy-start.29
  44.6 18.3 copy-start.33
  78.3 42.8 %copy-start.3 = (f32[3072,256]{0,1:T(8,128)}, f32[3072,256]{0,1:T(8,128)S(1)}, u32[]{:S(2)}) copy-start(f32[3072,256]{0,1:T(8,128)S(1)} %get-tuple-element.64) | copy-start | bytes 9437188
  78.3 52.3 %copy-start.22 = (f32[3072,2]{0,1:T(2,128)}, f32[3072,2]{0,1:T(2,128)S(1)}, u32[]{:S(2)}) copy-start(f32[3072,2]{0,1:T(2,128)S(1)} %add_rsqrt_fusion.1) | copy-start | bytes 73732
  78.3 52.3 %copy-start.49 = (f32[128]{0:T(128)}, f32[128]{0:T(128)S(1)}, u32[]{:S(2)}) copy-start(f32[128]{0:T(128)S(1)} %convert_element_type.204) | copy-start | bytes 1540
  83.8 54.5 %copy-start.31 = (f32[6,512]{1,0:T(8,128)}, f32[6,512]{1,0:T(8,128)S(1)}, u32[]{:S(2)}) copy-start(f32[6,512]{1,0:T(8,128)S(1)} %convert_element_type.197) | copy-start | bytes 36868
  83.8 177.1 %copy-start.43 = (f32[128]{0:T(128)}, f32[128]{0:T(128)S(1)}, u32[]{:S(2)}) copy-start(f32[128]{0:T(128)S(1)} %convert_element_type.196) | copy-start | bytes 1540
  237.3 24.3 copy-start.1
  237.3 24.3 copy-start.6
  261.6 22.7 copy-start.28
  284.3 34.5 %copy-start.15 = (bf16[6,512,2,128]{3,2,1,0:T(2,128)(2,1)S(1)}, bf16[6,512,2,128]{3,2,1,0:T(2,128)(2,1)}, u32[]{:S(2)}) copy-start(bf16[6,512,2,128]{3,2,1,0:T(2,128)(2,1)} %reshape.280) | copy-start | bytes 4718596
  318.7 29.0 copy-start.62
  384.0 23.8 copy-start.46
  407.7 98.7 %copy-start.37 = (f32[3072]{0:T(1024)}, f32[3072]{0:T(1024)S(1)}, u32[]{:S(2)}) copy-start(f32[3072]{0:T(1024)S(1)} %add_rsqrt_fusion.3) | copy-start | bytes 36868
  632.9 101.3 %copy-start.32 = (f32[6,512]{1,0:T(8,128)S(1)}, f32[6,512]{1,0:T(8,128)}, u32[]{:S(2)}) copy-start(f32[6,512]{1,0:T(8,128)} %copy-done.31) | copy-start | bytes 36868
  632.9 101.3 %copy-start.54 = (f32[64]{0:T(128)S(1)}, f32[64]{0:T(128)}, u32[]{:S(2)}) copy-start(f32[64]{0:T(128)} %copy-done.53) | copy-start | bytes 772
  731.7 22.5 copy-start.60
  731.7 22.7 copy-start.61
  731.7 285.5 %all-gather.23.cloned.1.call-start = ((), (), s32[]{:S(2)}) async-start(), calls=%async_computation.13 | async-start | bytes 30965760 | tf_op jit(solution)/shard_map/all_gather | solution.py:151
  732.5 393.7 %all-gather.25.cloned.1.call-start = ((), (), s32[]{:S(2)}) async-start(), calls=%async_computation.14 | async-start | bytes 30965760 | tf_op jit(solution)/shard_map/all_gather | solution.py:151
  733.2 518.5 %all-gather.27.cloned.1.call-start = ((), (), s32[]{:S(2)}) async-start(), calls=%async_computation.15 | async-start | bytes 5308416 | tf_op jit(solution)/shard_map/all_gather | solution.py:151
  734.0 1507.3 %all-gather.29.cloned.1.call-start = ((), (), s32[]{:S(2)}) async-start(), calls=%async_computation.16 | async-start | bytes 5308416 | tf_op jit(solution)/shard_map/all_gather | solution.py:151
  779.2 1545.7 %reduce-scatter.10.cloned.1.call-start = ((), (), s32[]{:S(2)}) async-start(), calls=%async_computation.18 | async-start | bytes 1769472 | tf_op jit(solution)/shard_map/reduce_scatter | solution.py:163
  1017.3 109.0 %copy-start.38 = (f32[3072]{0:T(1024)S(1)}, f32[3072]{0:T(1024)}, u32[]{:S(2)}) copy-start(f32[3072]{0:T(1024)} %copy-done.37) | copy-start | bytes 36868
  1017.3 109.0 %copy-start.41 = (f32[1536]{0:T(1024)S(1)}, f32[1536]{0:T(1024)}, u32[]{:S(2)}) copy-start(f32[1536]{0:T(1024)} %convert_element_type.226) | copy-start | bytes 18436
  1272.8 35.2 %copy-start.16 = (bf16[6,512,2,128]{3,2,1,0:T(2,128)(2,1)S(1)}, bf16[6,512,2,128]{3,2,1,0:T(2,128)(2,1)}, u32[]{:S(2)}) copy-start(bf16[6,512,2,128]{3,2,1,0:T(2,128)(2,1)} %reshape.280) | copy-start | bytes 4718596
  1308.1 29.8 %copy-start.21 = (bf16[6,512,2,128,1]{1,3,4,2,0:T(8,128)(2,1)S(1)}, bf16[6,512,2,128,1]{1,3,4,2,0:T(8,128)(2,1)}, u32[]{:S(2)}) copy-start(bf16[6,512,2,128,1]{1,3,4,2,0:T(8,128)(2,1)} %fusion.84) | copy-start | bytes 4718596
  1308.1 29.8 %copy-start.63 = (f32[6,2,512,6]{2,3,1,0:T(8,128)S(1)}, f32[6,2,512,6]{2,3,1,0:T(8,128)}, u32[]{:S(2)}) copy-start(f32[6,2,512,6]{2,3,1,0:T(8,128)} %copy-done.62) | copy-start | bytes 442372
  1546.5 25.1 copy-start.4
  1622.4 18.2 copy-start.2
  1622.4 18.2 copy-start.23
  1622.4 18.2 copy-start.51
  1631.7 25.1 copy-start.8
  1631.7 25.1 copy-start.55
  1669.8 29.3 copy-start.20
  1669.8 29.3 copy-start.45
  1699.1 625.8 %reduce-scatter.12.cloned.1.call-start = ((), (), s32[]{:S(2)}) async-start(), calls=%async_computation.19 | async-start | bytes 1769472 | tf_op jit(solution)/shard_map/reduce_scatter | solution.py:163
  1699.2 49.2 %slice-start = ((s8[18874368]{0:T(1024)(128)(4,1)}), s8[4194304]{0:T(1024)(128)(4,1)S(1)}, s32[]{:S(2)}) async-start(s8[18874368]{0:T(1024)(128)(4,1)} %bitcast.210), calls=%async_computation.24 | async-start | bytes 8388608
  1699.2 49.2 %slice-start.1 = ((s8[18874368]{0:T(1024)(128)(4,1)}), s8[4194304]{0:T(1024)(128)(4,1)S(1)}, s32[]{:S(2)}) async-start(s8[18874368]{0:T(1024)(128)(4,1)} %bitcast.210), calls=%async_computation.25 | async-start | bytes 8388608
  1699.2 49.2 %slice-start.2 = ((s8[18874368]{0:T(1024)(128)(4,1)}), s8[2097152]{0:T(1024)(128)(4,1)S(1)}, s32[]{:S(2)}) async-start(s8[18874368]{0:T(1024)(128)(4,1)} %bitcast.210), calls=%async_computation.26 | async-start | bytes 4194304
  1726.0 22.4 slice-start.3
  1726.0 22.4 slice-start.4
  1811.4 28.2 copy-start.11
  1819.5 505.4 %reduce-scatter.8.cloned.1.call-start = ((), (), s32[]{:S(2)}) async-start(), calls=%async_computation.17 | async-start | bytes 10616832 | tf_op jit(solution)/shard_map/reduce_scatter | solution.py:163
  1862.3 462.6 %reduce-scatter.14.cloned.1.call-start = ((), (), s32[]{:S(2)}) async-start(), calls=%async_computation.20 | async-start | bytes 10616832 | tf_op jit(solution)/shard_map/reduce_scatter | solution.py:163
  1886.6 438.4 %reduce-scatter.20.cloned.1.call-start = ((), (), s32[]{:S(2)}) async-start(), calls=%async_computation.23 | async-start | bytes 61931520 | tf_op jit(solution)/shard_map/reduce_scatter | solution.py:163
  1983.8 649.8 %reduce-scatter.18.cloned.1.call-start = ((), (), s32[]{:S(2)}) async-start(), calls=%async_computation.22 | async-start | bytes 61931520 | tf_op jit(solution)/shard_map/reduce_scatter | solution.py:163
  2084.8 858.3 %reduce-scatter.16.cloned.1.call-start = ((), (), s32[]{:S(2)}) async-start(), calls=%async_computation.21 | async-start | bytes 61931520 | tf_op jit(solution)/shard_map/reduce_scatter | solution.py:163
  2185.2 20.7 copy-start.27
  2185.2 39.9 %copy-start.57 = (f32[128]{0:T(128)S(1)}, f32[128]{0:T(128)}, u32[]{:S(2)}) copy-start(f32[128]{0:T(128)} %get-tuple-element.33) | copy-start | bytes 1540
  2185.2 39.9 %copy-start.56 = (f32[128]{0:T(128)S(1)}, f32[128]{0:T(128)}, u32[]{:S(2)}) copy-start(f32[128]{0:T(128)} %get-tuple-element.39) | copy-start | bytes 1540
  2185.2 39.9 %copy-start.14 = (bf16[3072,256]{0,1:T(8,128)(2,1)S(1)}, bf16[3072,256]{0,1:T(8,128)(2,1)}, u32[]{:S(2)}) copy-start(bf16[3072,256]{0,1:T(8,128)(2,1)} %copy-done.13) | copy-start | bytes 4718596
  2185.2 48.0 %copy-start.12 = (bf16[6,512,2,128]{3,2,1,0:T(2,128)(2,1)S(1)}, bf16[6,512,2,128]{3,2,1,0:T(2,128)(2,1)}, u32[]{:S(2)}) copy-start(bf16[6,512,2,128]{3,2,1,0:T(2,128)(2,1)} %copy-done.11) | copy-start | bytes 4718596
  2225.1 16.1 copy-start.34
  2241.2 38.2 %copy-start.48 = (f32[1536]{0:T(1024)S(1)}, f32[1536]{0:T(1024)}, u32[]{:S(2)}) copy-start(f32[1536]{0:T(1024)} %get-tuple-element.35) | copy-start | bytes 18436
  (22 other events, 167.1 us)
Sparse Core Ops, SparseCore 0:
  9.8 37.0 all-gather.10
  48.7 35.4 all-gather.12
  86.1 134.5 all-gather.14
  222.3 129.5 all-gather.16
  353.6 129.5 all-gather.18
  731.8 131.4 all-gather.20
  865.1 129.5 all-gather.22
  996.6 129.5 all-gather.24
  1128.1 33.2 all-gather.26
  1163.0 33.2 all-gather.28
  1699.2 29.9 reduce-scatter.9
  1819.6 29.9 reduce-scatter.11
  1862.4 68.5 reduce-scatter.7
  1934.9 68.4 reduce-scatter.13
  2007.3 316.7 reduce-scatter.19
  2328.1 305.4 reduce-scatter.17
  2637.6 305.5 reduce-scatter.15
where the time goes:
time: 2960 us; the launch traced here: 2950 us
  matrix products  1500 us (51%)
  waiting for transfers between devices  720 us (24%)
  local copies, waits for them, and re-layouts  311 us (11%)
  other arithmetic  242 us (8%)
  blocking collectives  161 us (5%)
    reduce_scatter x7, waiting for transfers between devices, device_step(): lax.psum_scatter(row_grad * inv_tokens, axis_name, scatter_dimension=0, t...  618 us
    dot_general x7, matrix products, matmul_nt(): lax.dot_general(left_op, right_op, (((1,), (1,)), ((), ())), preferred_el...  430 us
    dot_general x7, matrix products, matmul(): return jnp.dot(left_op, right_op, preferred_element_type=jnp.float32)  382 us
    dot_general x7, matrix products, matmul_tn(): lax.dot_general(left_op, right_op, (((0,), (0,)), ((), ())), preferred_el...  357 us
    concatenate x11, local copies, waits for them, and re-layouts, rotate_half(): jnp.concatenate([-tensor[..., half_dim:], tensor[..., :half_dim]], axis=-1)  112 us
    dot_general x1, matrix products, backward_local(): jnp.einsum('bksgt,bskgd->btkd', d_scores, q_grouped, preferred_element_ty...  111 us
    dot_general x1, matrix products, backward_local(): jnp.einsum('bksgt,btkd->bskgd', d_scores, saved_acts['k_seq'], preferred_...  97.3 us
    all_gather x10, waiting for transfers between devices, gather_weights(): lax.all_gather(row_shard, axis_name, axis=0, tiled=True)  96.5 us
  transfers between devices with their start and end apart: 17, of which 4 were waited for; matrix products, arithmetic and copies ran while one was open for 66% of the time, Pallas kernels for 0%

commit v1 on v0

v1 whole, which is shorter than its diff:
```python
import functools

import jax
import jax.numpy as jnp
from jax import lax
from jax.experimental import pallas as pl
from jax.experimental.pallas import tpu as pltpu
from jax.sharding import Mesh
from jax.sharding import PartitionSpec as P


RMS_EPS = 1e-6
ROPE_THETA = 1000000.0
F32 = jnp.float32
BF16 = jnp.bfloat16


def rms_scale(tensor):
    return lax.rsqrt(jnp.mean(tensor * tensor, axis=-1, keepdims=True) + RMS_EPS)


def norm_backward(d_unit, unit_val, scale_val):
    return scale_val * (d_unit - unit_val * jnp.mean(d_unit * unit_val, axis=-1, keepdims=True))


def matmul(left_op, right_op):
    return jnp.dot(left_op, right_op, preferred_element_type=F32)


def matmul_tn(left_op, right_op):
    return lax.dot_general(left_op, right_op, (((0,), (0,)), ((), ())), preferred_element_type=F32)


def matmul_nt(left_op, right_op):
    return lax.dot_general(left_op, right_op, (((1,), (1,)), ((), ())), preferred_element_type=F32)


def rope_tables(positions, head_dim):
    inv_freq = ROPE_THETA ** (-2.0 * jnp.arange(head_dim // 2, dtype=F32) / head_dim)
    rope_angle = positions.reshape(-1, 1).astype(F32) * inv_freq
    cos_half = jnp.cos(rope_angle)
    sin_half = jnp.sin(rope_angle)
    return jnp.concatenate([cos_half, cos_half], axis=-1), jnp.concatenate([-sin_half, sin_half], axis=-1)


def head_forward(projected, gain_vec, cos_t, sin_t):
    heads_float = projected.astype(F32)
    head_scale = rms_scale(heads_float)
    head_unit = heads_float * head_scale
    scaled = head_unit * gain_vec
    rotated = scaled * cos_t + pltpu.roll(scaled, scaled.shape[-1] // 2, 1) * sin_t
    return rotated.astype(BF16), head_unit, head_scale


def head_backward(d_rotated, head_unit, head_scale, gain_vec, cos_t, sin_t):
    d_scaled = d_rotated * cos_t - pltpu.roll(d_rotated, d_rotated.shape[-1] // 2, 1) * sin_t
    d_gain = jnp.sum(d_scaled * head_unit, axis=0, keepdims=True)
    return norm_backward(d_scaled * gain_vec, head_unit, head_scale).astype(BF16), d_gain


def probs_t(keys, queries, head_dim):
    key_len, q_len = keys.shape[0], queries.shape[0]
    scores = matmul_nt(keys, queries)
    tail = scores[key_len - q_len:]
    row = lax.broadcasted_iota(jnp.int32, tail.shape, 0)
    col = lax.broadcasted_iota(jnp.int32, tail.shape, 1)
    tail = jnp.where(row <= col, tail, -1e30)
    scores = tail if key_len == q_len else jnp.concatenate([scores[:key_len - q_len], tail], axis=0)
    top = jnp.max(scores, axis=0, keepdims=True)
    expo = jnp.exp((scores - top) * (head_dim ** -0.5))
    return expo * (1.0 / jnp.sum(expo, axis=0, keepdims=True))


def attention_forward_kernel(group, head_dim, q_tile, qkv_ref, cos_ref, sin_ref, qg_ref, kg_ref, ctx_ref):
    seq_len = qkv_ref.shape[0]
    cos_t, sin_t = cos_ref[...], sin_ref[...]
    base = group * head_dim
    k_rot, _, _ = head_forward(qkv_ref[:, base:base + head_dim], kg_ref[...], cos_t, sin_t)
    v_t = qkv_ref[:, base + head_dim:base + 2 * head_dim].T
    for head in range(group):
        lanes = slice(head * head_dim, (head + 1) * head_dim)
        q_rot, _, _ = head_forward(qkv_ref[:, lanes], qg_ref[...], cos_t, sin_t)
        for start in range(0, seq_len, q_tile):
            stop = start + q_tile
            probs = probs_t(k_rot[:stop], q_rot[start:stop], head_dim).astype(BF16)
            ctx_ref[start:stop, lanes] = matmul(v_t[:, :stop], probs).T.astype(BF16)


def attention_backward_kernel(group, head_dim, q_tile, qkv_ref, cos_ref, sin_ref, qg_ref, kg_ref, dctx_ref, dqkv_ref, gain_ref, dk_acc, dv_acc):
    seq_len = qkv_ref.shape[0]
    cos_t, sin_t = cos_ref[...], sin_ref[...]
    base = group * head_dim
    k_rot, k_unit, k_scale = head_forward(qkv_ref[:, base:base + head_dim], kg_ref[...], cos_t, sin_t)
    v_seq = qkv_ref[:, base + head_dim:base + 2 * head_dim]
    k_t = k_rot.T
    dk_acc[...] = jnp.zeros_like(dk_acc)
    dv_acc[...] = jnp.zeros_like(dv_acc)
    q_gain_sum = jnp.zeros((1, head_dim), F32)
    for head in range(group):
        lanes = slice(head * head_dim, (head + 1) * head_dim)
        q_rot, q_unit, q_scale = head_forward(qkv_ref[:, lanes], qg_ref[...], cos_t, sin_t)
        dq_tiles = []
        for start in range(0, seq_len, q_tile):
            stop = start + q_tile
            q_blk = q_rot[start:stop]
            d_out = dctx_ref[start:stop, lanes]
            probs = probs_t(k_rot[:stop], q_blk, head_dim)
            dv_acc[:stop, :] += matmul(probs.astype(BF16), d_out)
            d_probs = matmul_nt(v_seq[:stop], d_out)
            dot_row = jnp.sum(probs * d_probs, axis=0, keepdims=True)
            d_scores = (probs * (d_probs - dot_row) * (head_dim ** -0.5)).astype(BF16)
            dk_acc[:stop, :] += matmul(d_scores, q_blk)
            dq_tiles.append(matmul(k_t[:, :stop], d_scores).T)
        d_proj, d_gain = head_backward(jnp.concatenate(dq_tiles, axis=0), q_unit, q_scale, qg_ref[...], cos_t, sin_t)
        dqkv_ref[:, lanes] = d_proj
        q_gain_sum += d_gain
    d_proj, k_gain_sum = head_backward(dk_acc[...], k_unit, k_scale, kg_ref[...], cos_t, sin_t)
    dqkv_ref[:, base:base + head_dim] = d_proj
    dqkv_ref[:, base + head_dim:base + 2 * head_dim] = dv_acc[...].astype(BF16)

    @pl.when((pl.program_id(0) == 0) & (pl.program_id(1) == 0))
    def _():
        gain_ref[...] = jnp.zeros_like(gain_ref)

    gain_ref[0:1, :] += q_gain_sum
    gain_ref[1:2, :] += k_gain_sum


def norm_split_kernel(flag_ref, x_ref, attn_ref, gain_ref, resid_ref, scale_ref, norm_ref, own_ref, other_ref):
    resid = (x_ref[...].astype(F32) + attn_ref[...].astype(F32)).astype(BF16)
    resid_ref[...] = resid
    resid_float = resid.astype(F32)
    scale = rms_scale(resid_float)
    scale_ref[...] = jnp.broadcast_to(scale, scale_ref.shape)
    normed = (resid_float * scale * gain_ref[...]).astype(BF16)
    norm_ref[...] = normed
    first = flag_ref[0] == 0
    low = lax.broadcasted_iota(jnp.int32, (normed.shape[0], 128), 1) < 64
    for pair in range(normed.shape[1] // 768):
        tiles = [normed[:, pair * 768 + i * 128:pair * 768 + (i + 1) * 128].astype(F32) for i in range(6)]
        turned = [pltpu.roll(tile, 64, 1) for tile in tiles]
        even = [tiles[0], jnp.where(low, tiles[1], turned[3]), jnp.where(low, turned[3], turned[4])]
        odd = [jnp.where(low, turned[1], turned[2]), jnp.where(low, turned[2], tiles[4]), tiles[5]]
        for i in range(3):
            lanes = slice(pair * 384 + i * 128, pair * 384 + (i + 1) * 128)
            own_ref[:, lanes] = jnp.where(first, even[i], odd[i]).astype(BF16)
            other_ref[:, lanes] = jnp.where(first, odd[i], even[i]).astype(BF16)


def norm_split(core, x_flat, attn_out, gain, row_tile):
    tokens, width = x_flat.shape
    wide = pl.BlockSpec((row_tile, width), lambda i: (i, 0))
    half = pl.BlockSpec((row_tile, width // 2), lambda i: (i, 0))
    return pl.pallas_call(
        norm_split_kernel,
        out_shape=(
            jax.ShapeDtypeStruct((tokens, width), BF16),
            jax.ShapeDtypeStruct((tokens, 128), F32),
            jax.ShapeDtypeStruct((tokens, width), BF16),
            jax.ShapeDtypeStruct((tokens, width // 2), BF16),
            jax.ShapeDtypeStruct((tokens, width // 2), BF16),
        ),
        grid=(tokens // row_tile,),
        in_specs=[pl.BlockSpec(memory_space=pltpu.SMEM), wide, wide, pl.BlockSpec((1, width), lambda i: (0, 0))],
        out_specs=(wide, pl.BlockSpec((row_tile, 128), lambda i: (i, 0)), wide, half, half),
        compiler_params=pltpu.CompilerParams(dimension_semantics=("arbitrary",), vmem_limit_bytes=40 * 1024 * 1024),
        cost_estimate=pl.CostEstimate(flops=20 * tokens * width, bytes_accessed=10 * tokens * width, transcendentals=tokens),
        name="norm_split",
    )(core, x_flat, attn_out, gain)


def attention_specs(seq_len, group, head_dim):
    width = (group + 2) * head_dim
    return [
        pl.BlockSpec((seq_len, width), lambda b, k: (b, k)),
        pl.BlockSpec((seq_len, head_dim), lambda b, k: (b, 0)),
        pl.BlockSpec((seq_len, head_dim), lambda b, k: (b, 0)),
        pl.BlockSpec((1, head_dim), lambda b, k: (0, 0)),
        pl.BlockSpec((1, head_dim), lambda b, k: (0, 0)),
    ]


def attention_forward(qkv, cos_t, sin_t, q_gain, k_gain, batch, group, kv_heads, head_dim, q_tile):
    tokens = qkv.shape[0]
    seq_len = tokens // batch
    flops = 3 * tokens * seq_len * kv_heads * group * head_dim
    return pl.pallas_call(
        functools.partial(attention_forward_kernel, group, head_dim, q_tile),
        out_shape=jax.ShapeDtypeStruct((tokens, kv_heads * group * head_dim), BF16),
        grid=(batch, kv_heads),
        in_specs=attention_specs(seq_len, group, head_dim),
        out_specs=pl.BlockSpec((seq_len, group * head_dim), lambda b, k: (b, k)),
        compiler_params=pltpu.CompilerParams(dimension_semantics=("arbitrary", "arbitrary"), vmem_limit_bytes=40 * 1024 * 1024),
        cost_estimate=pl.CostEstimate(flops=flops, bytes_accessed=4 * qkv.size, transcendentals=tokens * seq_len * kv_heads * group),
        name="attn_fwd",
    )(qkv, cos_t, sin_t, q_gain, k_gain)


def attention_backward(qkv, cos_t, sin_t, q_gain, k_gain, d_ctx, batch, group, kv_heads, head_dim, q_tile):
    tokens = qkv.shape[0]
    seq_len = tokens // batch
    flops = 8 * tokens * seq_len * kv_heads * group * head_dim
    return pl.pallas_call(
        functools.partial(attention_backward_kernel, group, head_dim, q_tile),
        out_shape=(jax.ShapeDtypeStruct(qkv.shape, BF16), jax.ShapeDtypeStruct((8, head_dim), F32)),
        grid=(batch, kv_heads),
        in_specs=attention_specs(seq_len, group, head_dim) + [pl.BlockSpec((seq_len, group * head_dim), lambda b, k: (b, k))],
        out_specs=(pl.BlockSpec((seq_len, (group + 2) * head_dim), lambda b, k: (b, k)), pl.BlockSpec((8, head_dim), lambda b, k: (0, 0))),
        scratch_shapes=[pltpu.VMEM((seq_len, head_dim), F32)] * 2,
        compiler_params=pltpu.CompilerParams(dimension_semantics=("arbitrary", "arbitrary"), vmem_limit_bytes=40 * 1024 * 1024),
        cost_estimate=pl.CostEstimate(flops=flops, bytes_accessed=8 * qkv.size, transcendentals=tokens * seq_len * kv_heads * group),
        name="attn_bwd",
    )(qkv, cos_t, sin_t, q_gain, k_gain, d_ctx)


def solution(mesh):
    chips = mesh.devices.size // 2
    pair_mesh = Mesh(mesh.devices.reshape(chips, 2), ("chip", "core"))
    both = ("chip", "core")
    sharded = P(both)
    in_specs = (sharded, sharded, sharded, sharded, sharded, P(), P()) + (sharded,) * 7
    out_specs = (sharded, sharded, sharded, sharded, P(), P()) + (sharded,) * 7
    swap = [(0, 1), (1, 0)]

    def gather(shard):
        return lax.all_gather(shard, both, axis=0, tiled=True)

    def scatter(part, axes):
        return lax.psum_scatter(part, axes, scatter_dimension=0, tiled=True)

    def sum_all(values):
        values = values + lax.ppermute(values, "core", swap)
        step = 1
        while step < chips:
            values = values + lax.ppermute(values, "chip", [(c, c ^ step) for c in range(chips)])
            step *= 2
        return values

    def device_step(hidden, grad_out, positions, norm1_gain, norm2_gain, q_norm_gain, k_norm_gain, w_q, w_k, w_v, w_o, w_gate, w_up, w_down):
        batch, seq_len, width = hidden.shape
        head_dim = q_norm_gain.shape[0]
        kv_heads = w_k.shape[1] // head_dim
        group = w_q.shape[1] // head_dim // kv_heads
        tokens = batch * seq_len
        rows = w_q.shape[0]
        core = lax.axis_index("core")
        first = core == 0
        device = lax.axis_index("chip") * 2 + core
        inv_tokens = 1.0 / (tokens * chips * 2)
        q_tile = 256

        def own(even, odd):
            return jnp.where(first, even, odd)

        pieces = []
        for head in range(kv_heads):
            pieces.append(w_q[:, head * group * head_dim:(head + 1) * group * head_dim])
            pieces.append(w_k[:, head * head_dim:(head + 1) * head_dim])
            pieces.append(w_v[:, head * head_dim:(head + 1) * head_dim])
        qkv_width = kv_heads * (group + 2) * head_dim
        pieces.append(jnp.pad(jnp.stack([norm1_gain, norm2_gain], axis=1), ((0, 0), (0, head_dim - 2))))
        qkv_full = gather(jnp.concatenate(pieces, axis=1))
        wo_full = gather(w_o)
        gate_full = gather(w_gate)
        up_full = gather(w_up)
        down_full = gather(w_down)
        w_qkv = qkv_full[:, :qkv_width]
        gain1 = qkv_full[:, qkv_width].astype(F32)
        gain2 = qkv_full[:, qkv_width + 1].astype(F32)
        q_gain = q_norm_gain.astype(F32).reshape(1, head_dim)
        k_gain = k_norm_gain.astype(F32).reshape(1, head_dim)

        x_float = hidden.reshape(tokens, width).astype(F32)
        dy = grad_out.reshape(tokens, width)
        x_scale = rms_scale(x_float)
        normed = (x_float * x_scale * gain1).astype(BF16)
        qkv = matmul(normed, w_qkv).astype(BF16)
        cos_t, sin_t = rope_tables(positions, head_dim)
        ctx = attention_forward(qkv, cos_t, sin_t, q_gain, k_gain, batch, group, kv_heads, head_dim, q_tile)
        attn_out = matmul(ctx, wo_full).astype(BF16)
        resid, r_wide, mlp_in, in_own, in_other = norm_split(core.reshape(1), hidden.reshape(tokens, width), attn_out, gain2.reshape(1, width), 256)
        resid_float = resid.astype(F32)
        r_scale = r_wide[:, :1]
        gate_proj = matmul(mlp_in, gate_full).astype(BF16)
        up_proj = matmul(mlp_in, up_full).astype(BF16)
        mlp_act = (jax.nn.silu(gate_proj.astype(F32)) * up_proj.astype(F32)).astype(BF16)

        half = width // 2
        dy_own, dy_other = own(dy[:, :half], dy[:, half:]), own(dy[:, half:], dy[:, :half])
        down_recv = lax.ppermute(matmul_tn(mlp_act, dy_other), "core", swap)
        down_proj = matmul(mlp_act, down_full).astype(BF16)
        layer_out = (resid_float + down_proj.astype(F32)).astype(BF16)
        dy_own, layer_out = lax.optimization_barrier((dy_own, layer_out))
        down_pair = (matmul_tn(mlp_act, dy_own) + down_recv) * inv_tokens
        down_rows = scatter(down_pair, "chip")
        drows = down_rows.shape[0] // 2
        down_back = lax.ppermute(own(down_rows[drows:], down_rows[:drows]), "core", swap)
        down_mine = own(down_rows[:drows], down_rows[drows:])
        g_down = own(jnp.concatenate([down_mine, down_back], axis=1), jnp.concatenate([down_back, down_mine], axis=1))

        dy_late, layer_out, _ = lax.optimization_barrier((dy, layer_out, down_pair))
        d_mlp_act = matmul_nt(dy_late, down_full)
        gate_float = gate_proj.astype(F32)
        gate_sig = jax.nn.sigmoid(gate_float)
        d_up = (d_mlp_act * gate_float * gate_sig).astype(BF16)
        d_gate = (d_mlp_act * up_proj.astype(F32) * gate_sig * (1.0 + gate_float * (1.0 - gate_sig))).astype(BF16)

        gate_recv = lax.ppermute(matmul_tn(in_other, d_gate), "core", swap)
        up_recv = lax.ppermute(matmul_tn(in_other, d_up), "core", swap)
        gate_pair = (matmul_tn(in_own, d_gate) + gate_recv) * inv_tokens
        up_pair = (matmul_tn(in_own, d_up) + up_recv) * inv_tokens
        g_gate = scatter(gate_pair, "chip")
        g_up = scatter(up_pair, "chip")
        d_gate, d_up, _, _ = lax.optimization_barrier((d_gate, d_up, gate_pair, up_pair))

        d_mlp_in = matmul_nt(d_gate, gate_full) + matmul_nt(d_up, up_full)
        r_unit = resid_float * r_scale
        grad_norm2 = jnp.sum(d_mlp_in * r_unit, axis=0)
        d_resid = dy.astype(F32) + norm_backward(d_mlp_in * gain2, r_unit, r_scale)
        d_resid_bf = d_resid.astype(BF16)
        wo_part = matmul_tn(ctx, d_resid_bf) * inv_tokens
        g_wo = scatter(wo_part, both)
        d_resid_bf, _ = lax.optimization_barrier((d_resid_bf, wo_part))
        d_ctx = matmul_nt(d_resid_bf, wo_full).astype(BF16)
        d_qkv, gain_sums = attention_backward(qkv, cos_t, sin_t, q_gain, k_gain, d_ctx, batch, group, kv_heads, head_dim, q_tile)
        g_qkv = scatter(matmul_tn(normed, d_qkv) * inv_tokens, both)

        d_normed = matmul_nt(d_qkv, w_qkv)
        x_unit = x_float * x_scale
        grad_norm1 = jnp.sum(d_normed * x_unit, axis=0)
        d_hidden = (d_resid + norm_backward(d_normed * gain1, x_unit, x_scale)).astype(BF16)

        small = jnp.concatenate([grad_norm1, grad_norm2, gain_sums[0], gain_sums[1]]) * inv_tokens
        small = sum_all(small.reshape(-1, 128)).reshape(-1)
        g_norm1 = lax.dynamic_slice_in_dim(small[:width], device * rows, rows)
        g_norm2 = lax.dynamic_slice_in_dim(small[width:2 * width], device * rows, rows)
        g_qgain = small[2 * width:2 * width + head_dim]
        g_kgain = small[2 * width + head_dim:]

        qs, ks, vs = [], [], []
        for head in range(kv_heads):
            start = head * (group + 2) * head_dim
            qs.append(g_qkv[:, start:start + group * head_dim])
            ks.append(g_qkv[:, start + group * head_dim:start + (group + 1) * head_dim])
            vs.append(g_qkv[:, start + (group + 1) * head_dim:start + (group + 2) * head_dim])
        g_wq, g_wk, g_wv = (jnp.concatenate(part, axis=1) for part in (qs, ks, vs))
        return (layer_out.reshape(hidden.shape), d_hidden.reshape(hidden.shape), g_norm1, g_norm2, g_qgain, g_kgain, g_wq, g_wk, g_wv, g_wo, g_gate, g_up, g_down)

    return jax.shard_map(device_step, mesh=pair_mesh, in_specs=in_specs, out_specs=out_specs, check_vma=False)
```

time: 2960 us -> 2100 us (0.71)
  matrix products: 1500 us -> 1140 us
  local copies, waits for them, and re-layouts: 311 us -> 25.2 us
  Pallas kernels: 0 us -> 181 us
  other arithmetic: 242 us -> 78.6 us
  blocking collectives: 161 us -> 0 us
  waiting for transfers between devices: 720 us -> 652 us
    dot_general x12 -> x5, matrix products: 679 us -> 370 us  [matmul(): return jnp.dot(left_op, right_op, preferred_element_type=F32)]
    pallas_call x0 -> x3, Pallas kernels: none -> 181 us  [the longest x1 110 us: attention_backward(): pl.pallas_call(functools.partial(attention_backward_kernel, group, head_d...]
    concatenate x12 -> x1, local copies, waits for them, and re-layouts: 114 us -> 0.02 us  [device_step(): qkv_full = gather(jnp.concatenate(pieces, axis=1))]
    all_gather x4 -> x0, blocking collectives: 87 us -> none  [gather_weights(): lax.all_gather(row_shard, axis_name, axis=0, tiled=True)]
    reshape x6 -> x0, local copies, waits for them, and re-layouts: 84.6 us -> none  [the longest x2 35.2 us: backward_local(): matmul_nt(d_resid_bf, w_o).astype(jnp.bfloat16)]
    unnamed x3 -> x0, blocking collectives: 73.6 us -> none
    reduce_scatter x7 -> x5, waiting for transfers between devices: 618 us -> 549 us  [scatter(): return lax.psum_scatter(part, axes, scatter_dimension=0, tiled=True)]
    convert_element_type x14 -> x4, other arithmetic: 93.5 us -> 44.1 us  [the longest x1 28.1 us: device_step(): (d_resid + norm_backward(d_normed * gain1, x_unit, x_scale)).astype(BF16)]
  transfers between devices with their start and end apart: 17 -> 17, of which waited for: 4 -> 9; matrix products, arithmetic and copies ran while one was open for 66% -> 46% of each run, Pallas kernels for 0% -> 9%
where the time goes in v1:
time: 2100 us; the launch traced here: 2090 us
  matrix products  1140 us (54%)
  waiting for transfers between devices  652 us (31%)
  Pallas kernels  181 us (9%)
  other arithmetic  78.6 us (4%)
  local copies, waits for them, and re-layouts  25.2 us (1%)
    reduce_scatter x5, waiting for transfers between devices, scatter(): return lax.psum_scatter(part, axes, scatter_dimension=0, tiled=True)  549 us
    dot_general x5, matrix products, matmul_nt(): lax.dot_general(left_op, right_op, (((1,), (1,)), ((), ())), preferred_el...  402 us
    dot_general x5, matrix products, matmul(): return jnp.dot(left_op, right_op, preferred_element_type=F32)  370 us
    dot_general x8, matrix products, matmul_tn(): lax.dot_general(left_op, right_op, (((0,), (0,)), ((), ())), preferred_el...  364 us
    pallas_call x1, Pallas kernels, attention_backward(): pl.pallas_call(functools.partial(attention_backward_kernel, group, head_d...  110 us
    all_gather x5, waiting for transfers between devices, gather(): return lax.all_gather(shard, both, axis=0, tiled=True)  95.8 us
    pallas_call x1, Pallas kernels, attention_forward(): pl.pallas_call(functools.partial(attention_forward_kernel, group, head_di...  53.1 us
  transfers between devices with their start and end apart: 17, of which 9 were waited for; matrix products, arithmetic and copies ran while one was open for 46% of the time, Pallas kernels for 9%

profile of v1, /device:TPU:0, one launch (start us, length us, event | category | flops | bytes accessed | tf_op | source)
XLA Modules:
  0.0 2092.5 jit_solution(6353135569899603614)
XLA Ops:
  7.2 0.7 stack.9
  7.9 0.7 stack.10
  8.7 1.0 slice_dynamic-update-slice_fusion.1
  9.7 0.8 slice_dynamic-update-slice_fusion.5
  10.5 0.8 slice_dynamic-update-slice_fusion.4
  11.4 1.0 slice_dynamic-update-slice_fusion
  12.3 0.8 slice_dynamic-update-slice_fusion.3
  13.2 0.8 slice_dynamic-update-slice_fusion.2
  14.0 0.9 copy-done.8
  15.0 0.7 all-gather.8.cloned.1.call-update
  15.7 0.7 all-gather.10.cloned.1.call-update
  17.7 0.7 convert_element_type.112
  18.4 5.8 multiply_reduce_fusion.2
  24.2 5.8 fusion.27
  30.1 6.5 broadcast_select_fusion
  36.5 0.9 pad_maximum_fusion
  37.4 22.0 %all-gather.6.cloned.1.call-done = bf16[1536,2176]{1,0:T(8,128)(2,1)} async-done(((bf16[192,2176]{1,0:T(8,128)(2,1)}), bf16[1536,2176]{1,0:T(8,128)(2,1)}) %all-gather.6.cloned.1.call-update) | async-done | bytes 6684688 | tf_op jit(solution)/shard_map/all_gather | solution.py:226
  59.4 1.6 convert_reduce_fusion
  61.6 26.1 %convolution_convert_fusion.4.qkv_ref = bf16[3072,2048]{1,0:T(8,128)(2,1)} fusion(bf16[1536,2176]{1,0:T(8,128)(2,1)} %all-gather.6.cloned.1.call-done, bf16[3072,1536]{1,0:T(8,128)(2,1)} %bitcast.72, f32[1536]{0:T(1024)S(1)} %get-tuple-element.46, f32[3072]{0:T(1024)S(1)} %rsqrt.12), kind=kOutput, calls=%fused_computation.41 | convolution fusion | flops 19352518656 | bytes 28329984 | tf_op jit(solution)/shard_map/dot_general | solution.py:27
  87.8 53.1 %attn_fwd.1 = bf16[3072,1536]{1,0:T(8,128)(2,1)S(1)} custom-call(bf16[3072,2048]{1,0:T(8,128)(2,1)} %convolution_convert_fusion.4.qkv_ref, f32[3072,128]{1,0:T(8,128)S(1)} %get-tuple-element.70.cos_ref, f32[3072,128]{1,0:T(8,128)S(1)} %get-tuple-element.71.sin_ref, f32[1,128]{1,0:T(1,128)S(1)} %get-tuple-element.73.qg_ref, f32[1,128]{1,0:T(1,128)S(1)} %get-tuple-element.72.kg_ref), custom_call_target="tpu_custom_call" | custom-call | flops 7247757312 | bytes 25165824 | tf_op jit(solution)/shard_map/attn_fwd/pallas_call | solution.py:187
  140.9 3.7 copy-done.5
  144.6 21.0 %convolution_convert_fusion.3.attn_ref = bf16[3072,1536]{1,0:T(8,128)(2,1)} fusion(bf16[3072,1536]{1,0:T(8,128)(2,1)} %copy-done.5, bf16[1536,1536]{1,0:T(8,128)(2,1)} %all-gather.8.cloned.1.call-done), kind=kOutput, calls=%fused_computation.40 | convolution fusion | flops 14500233216 | bytes 23592960 | tf_op jit(solution)/shard_map/dot_general | solution.py:27
  165.6 18.2 norm_split.1
  183.8 2.2 copy-done.2
  186.0 2.2 copy-done.3
  188.1 37.8 %all-gather.10.cloned.1.call-done = bf16[1536,8960]{1,0:T(8,128)(2,1)} async-done(((bf16[192,8960]{1,0:T(8,128)(2,1)}), bf16[1536,8960]{1,0:T(8,128)(2,1)}) %all-gather.10.cloned.1.call-update) | async-done | bytes 27525136 | tf_op jit(solution)/shard_map/all_gather | solution.py:226
  225.9 95.3 %convolution_convert_fusion.1 = bf16[3072,8960]{1,0:T(8,128)(2,1)} fusion(bf16[3072,1536]{1,0:T(8,128)(2,1)} %get-tuple-element.28, bf16[1536,8960]{1,0:T(8,128)(2,1)} %all-gather.10.cloned.1.call-done), kind=kOutput, calls=%fused_computation.17 | convolution fusion | flops 84584693760 | bytes 92012544 | tf_op jit(solution)/shard_map/dot_general | solution.py:27
  321.2 36.0 %all-gather.12.cloned.1.call-done = bf16[1536,8960]{1,0:T(8,128)(2,1)} async-done(((bf16[192,8960]{1,0:T(8,128)(2,1)}), bf16[1536,8960]{1,0:T(8,128)(2,1)}) %all-gather.12.cloned.1.call-update) | async-done | bytes 27525136 | tf_op jit(solution)/shard_map/all_gather | solution.py:226
  357.2 129.2 %fusion = (bf16[3072,8960]{1,0:T(8,128)(2,1)}, bf16[3072,8960]{1,0:T(8,128)(2,1)}) fusion(bf16[3072,8960]{1,0:T(8,128)(2,1)} %convolution_convert_fusion.1, bf16[3072,1536]{1,0:T(8,128)(2,1)} %get-tuple-element.28, bf16[1536,8960]{1,0:T(8,128)(2,1)} %all-gather.12.cloned.1.call-done), kind=kOutput, calls=%fused_computation.6 | convolution fusion | flops 84804894720 | bytes 202113024 | tf_op jit(solution)/shard_map/dot_general | solution.py:27
  486.4 54.0 %fusion.22 = f32[8960,768]{1,0:T(8,128)} fusion(bf16[3072,8960]{1,0:T(8,128)(2,1)} %get-tuple-element.66, pred[]{:T(512)S(6)} %eq.3, bf16[3072,1536]{1,0:T(8,128)(2,1)} %bitcast.70), kind=kOutput, calls=%fused_computation.49 | convolution fusion | flops 42280943616 | bytes 92012544 | tf_op jit(solution)/shard_map/dot_general | solution.py:31
  540.6 98.9 %fusion.18 = bf16[3072,1536]{1,0:T(8,128)(2,1)} fusion(bf16[3072,1536]{1,0:T(8,128)(2,1)} %get-tuple-element.27, bf16[3072,8960]{1,0:T(8,128)(2,1)} %get-tuple-element.66, bf16[8960,1536]{1,0:T(8,128)(2,1)} %all-gather.14.cloned.1.call-done), kind=kOutput, calls=%fused_computation.31 | convolution fusion | flops 84580761600 | bytes 101449728 | tf_op jit(solution)/shard_map/dot_general | solution.py:27
  639.5 53.9 %add_multiply_fusion.2 = f32[8960,768]{1,0:T(8,128)} fusion(f32[8960,768]{1,0:T(8,128)} %collective-permute-done, bf16[3072,8960]{1,0:T(8,128)(2,1)} %get-tuple-element.66, bf16[3072,768]{1,0:T(8,128)(2,1)} %broadcast_select_fusion), kind=kOutput, calls=%fused_computation.20 | convolution fusion | flops 42292346880 | bytes 114819072 | tf_op jit(solution)/shard_map/dot_general | solution.py:31
  693.3 152.4 %fusion.9 = (bf16[3072,8960]{1,0:T(8,128)(2,1)}, bf16[3072,8960]{1,0:T(8,128)(2,1)}) fusion(bf16[3072,8960]{1,0:T(8,128)(2,1)} %convolution_convert_fusion.1, bf16[3072,8960]{1,0:T(8,128)(2,1)} %get-tuple-element.67, bf16[3072,1536]{1,0:T(8,128)(2,1)} %bitcast.71, bf16[8960,1536]{1,0:T(8,128)(2,1)} %all-gather.14.cloned.1.call-done), kind=kOutput, calls=%fused_computation.15 | convolution fusion | flops 84970045440 | bytes 257163264 | tf_op jit(solution)/shard_map/dot_general | solution.py:35
  845.8 54.0 %fusion.32 = f32[768,8960]{1,0:T(8,128)} fusion(bf16[3072,768]{1,0:T(8,128)(2,1)} %copy-done.3, bf16[3072,8960]{1,0:T(8,128)(2,1)} %get-tuple-element.36), kind=kOutput, calls=%fused_computation.93 | convolution fusion | flops 42278584320 | bytes 87293952 | tf_op jit(solution)/shard_map/dot_general | solution.py:31
  900.1 50.1 %fusion.33 = f32[768,8960]{1,0:T(8,128)} fusion(bf16[3072,768]{1,0:T(8,128)(2,1)S(1)} %copy-done.4, bf16[3072,8960]{1,0:T(8,128)(2,1)} %get-tuple-element.37), kind=kOutput, calls=%fused_computation.94 | convolution fusion | flops 42278584320 | bytes 87293952 | tf_op jit(solution)/shard_map/dot_general | solution.py:31
  950.4 1.1 slice_reduce_fusion
  951.6 53.7 %add_multiply_fusion.1 = f32[768,8960]{1,0:T(8,128)} fusion(f32[768,8960]{1,0:T(8,128)} %collective-permute-done.1, bf16[3072,768]{1,0:T(8,128)(2,1)} %copy-done.2, bf16[3072,8960]{1,0:T(8,128)(2,1)} %get-tuple-element.36), kind=kOutput, calls=%fused_computation.19 | convolution fusion | flops 42292346880 | bytes 114819072 | tf_op jit(solution)/shard_map/dot_general | solution.py:31
  1005.3 53.1 %add_multiply_fusion = f32[768,8960]{1,0:T(8,128)} fusion(f32[768,8960]{1,0:T(8,128)} %collective-permute-done.2, bf16[3072,768]{1,0:T(8,128)(2,1)} %copy-done.2, bf16[3072,8960]{1,0:T(8,128)(2,1)} %get-tuple-element.37), kind=kOutput, calls=%fused_computation.18 | convolution fusion | flops 42292346880 | bytes 114819072 | tf_op jit(solution)/shard_map/dot_general | solution.py:31
  1058.4 96.8 %fusion.34 = f32[3072,1536]{1,0:T(8,128)} fusion(bf16[3072,8960]{1,0:T(8,128)(2,1)} %get-tuple-element.36, bf16[1536,8960]{1,0:T(8,128)(2,1)} %all-gather.10.cloned.1.call-done), kind=kOutput, calls=%fused_computation.95 | convolution fusion | flops 84557168640 | bytes 101449728 | tf_op jit(solution)/shard_map/dot_general | solution.py:35
  1155.2 104.6 %fusion.17 = (f32[1536]{0:T(1024)}, f32[3072]{0:T(1024)S(1)}, f32[3072,1536]{1,0:T(8,128)}) fusion(bf16[3072,1536]{1,0:T(8,128)(2,1)} %get-tuple-element.27, f32[3072]{0:T(1024)S(1)} %copy-done.11, f32[1536]{0:T(1024)S(1)} %copy-done.10, f32[3072,1536]{1,0:T(8,128)} %fusion.34, bf16[3072,8960]{1,0:T(8,128)(2,1)} %get-tuple-element.37, ...), kind=kOutput, calls=%fused_computation.30 | convolution fusion | flops 84594917376 | bytes 129798144 | tf_op jit(solution)/shard_map/dot_general | solution.py:35
  1259.8 13.7 fusion.29
  1273.5 3.5 copy-done.7
  1277.0 17.8 convolution_multiply_fusion.1
  1294.8 18.6 convolution_convert_fusion.2.dctx_ref
  1313.5 109.6 %attn_bwd.1 = (bf16[3072,2048]{1,0:T(8,128)(2,1)}, f32[8,128]{1,0:T(8,128)S(1)}) custom-call(bf16[3072,2048]{1,0:T(8,128)(2,1)} %convolution_convert_fusion.4.qkv_ref, f32[3072,128]{1,0:T(8,128)S(1)} %copy-done.1, f32[3072,128]{1,0:T(8,128)S(1)} %get-tuple-element.71.sin_ref, f32[1,128]{1,0:T(1,128)S(1)} %get-tuple-element.73.qg_ref, ...), custom_call_target="tpu_custom_call" | custom-call | flops 19327352832 | bytes 50331648 | tf_op jit(solution)/shard_map/attn_bwd/pallas_call | solution.py:203
  1423.2 27.5 %convolution_multiply_fusion = f32[1536,2048]{1,0:T(8,128)} fusion(bf16[3072,2048]{1,0:T(8,128)(2,1)} %get-tuple-element.39, bf16[3072,1536]{1,0:T(8,128)(2,1)} %bitcast.74, f32[1536]{0:T(1024)S(1)} %copy-done.16, f32[3072]{0:T(1024)S(1)} %copy-done.14), kind=kOutput, calls=%fused_computation.43 | convolution fusion | flops 19349372928 | bytes 34621440 | tf_op jit(solution)/shard_map/dot_general | solution.py:31
  1450.8 0.7 reduce-scatter.8.cloned.1.call-update
  1451.5 0.7 reduce-scatter.10.cloned.1.call-update
  1452.8 29.9 %multiply_reduce_fusion = (f32[1536]{0:T(1024)S(1)}, f32[3072]{0:T(1024)S(1)}, f32[3072,1536]{1,0:T(8,128)}) fusion(f32[3072]{0:T(1024)S(1)} %copy-done.14, bf16[6,512,1536]{2,1,0:T(8,128)(2,1)} %param.14, f32[1536]{0:T(1024)S(1)} %copy-done.16, bf16[3072,2048]{1,0:T(8,128)(2,1)} %get-tuple-element.39, bf16[1536,2176]{1,0:T(8,128)(2,1)} %all-gather.6.cloned.1.call-done), kind=kOutput, calls=%fused_computation.32 | convolution fusion | flops 19360378880 | bytes 47222784 | tf_op jit(solution)/shard_map/dot_general | solution.py:35
  1483.1 0.8 collective-permute-done.3
  1484.0 1.9 collective-permute-start.4
  1485.9 2.3 collective-permute-done.4
  1488.2 5.3 slice_select_fusion.1
  1493.5 28.1 %add_convert_fusion = bf16[3072,1536]{1,0:T(8,128)(2,1)} fusion(f32[3072,1536]{1,0:T(8,128)} %get-tuple-element.69, f32[3072]{0:T(1024)S(1)} %broadcast_multiply_fusion, f32[1536]{0:T(1024)S(1)} %copy-done.16, f32[3072]{0:T(1024)S(1)} %copy-done.14, bf16[6,512,1536]{2,1,0:T(8,128)(2,1)} %param.14, f32[3072]{0:T(1024)S(1)} %broadcast_multiply_fusion.1, ...), kind=kLoop, calls=%fused_computation.33 | loop fusion | flops 75497472 | bytes 75558912 | tf_op jit(solution)/shard_map/convert_element_type | solution.py:331
  1523.4 11.6 reduce-scatter.6.cloned.1.call-done
  1535.0 1.1 fusion.30
  1536.1 0.7 pad_maximum_fusion.4
  1536.8 0.7 pad_maximum_fusion.3
  1537.5 1.3 fusion.31
  1538.8 1.2 pad_maximum_fusion.2
  1540.0 7.7 maximum_select_fusion
  1547.6 59.9 %reduce-scatter.8.cloned.1.call-done = f32[192,1536]{1,0:T(8,128)} async-done(((f32[1536,1536]{1,0:T(8,128)}), f32[192,1536]{1,0:T(8,128)}) %reduce-scatter.8.cloned.1.call-update) | async-done | bytes 1179664 | tf_op jit(solution)/shard_map/reduce_scatter | solution.py:229
  1607.5 238.9 %reduce-scatter.10.cloned.1.call-done = f32[192,8960]{1,0:T(8,128)} async-done(((f32[768,8960]{1,0:T(8,128)}), f32[192,8960]{1,0:T(8,128)}) %reduce-scatter.10.cloned.1.call-update) | async-done | bytes 6881296 | tf_op jit(solution)/shard_map/reduce_scatter | solution.py:229
  1846.5 238.8 %reduce-scatter.12.cloned.1.call-done = f32[192,8960]{1,0:T(8,128)} async-done(((f32[768,8960]{1,0:T(8,128)}), f32[192,8960]{1,0:T(8,128)}) %reduce-scatter.12.cloned.1.call-update) | async-done | bytes 6881296 | tf_op jit(solution)/shard_map/reduce_scatter | solution.py:229
  (83 shorter events, 5.9 us)
Async XLA Ops:
  7.2 17.0 copy-start.17
  7.2 17.0 copy-start.18
  7.2 52.2 %all-gather.6.cloned.1.call-start = ((), (), s32[]{:S(2)}) async-start(), calls=%async_computation.5 | async-start | bytes 7520256 | tf_op jit(solution)/shard_map/all_gather | solution.py:226
  14.0 0.9 copy-start.8
  14.9 129.7 %all-gather.8.cloned.1.call-start = ((), (), s32[]{:S(2)}) async-start(), calls=%async_computation.6 | async-start | bytes 5308416 | tf_op jit(solution)/shard_map/all_gather | solution.py:226
  15.7 210.2 %all-gather.10.cloned.1.call-start = ((), (), s32[]{:S(2)}) async-start(), calls=%async_computation.7 | async-start | bytes 30965760 | tf_op jit(solution)/shard_map/all_gather | solution.py:226
  16.4 340.8 %all-gather.12.cloned.1.call-start = ((), (), s32[]{:S(2)}) async-start(), calls=%async_computation.8 | async-start | bytes 30965760 | tf_op jit(solution)/shard_map/all_gather | solution.py:226
  17.0 523.6 %all-gather.14.cloned.1.call-start = ((), (), s32[]{:S(2)}) async-start(), calls=%async_computation.9 | async-start | bytes 30965760 | tf_op jit(solution)/shard_map/all_gather | solution.py:226
  17.6 1470.6 %reduce-scatter.14.cloned.1.call-start = ((), (), s32[]{:S(2)}) async-start(), calls=%async_computation.14 | async-start | bytes 34406400 | tf_op jit(solution)/shard_map/reduce_scatter | solution.py:229
  24.2 63.6 %copy-start.13 = (f32[3072]{0:T(1024)}, f32[3072]{0:T(1024)S(1)}, u32[]{:S(2)}) copy-start(f32[3072]{0:T(1024)S(1)} %rsqrt.12) | copy-start | bytes 36868
  37.4 50.4 %copy-start = (f32[3072,128]{1,0:T(8,128)}, f32[3072,128]{1,0:T(8,128)S(1)}, u32[]{:S(2)}) copy-start(f32[3072,128]{1,0:T(8,128)S(1)} %get-tuple-element.70.cos_ref) | copy-start | bytes 4718596
  61.0 0.6 copy-start.9
  61.0 26.7 %copy-start.15 = (f32[1536]{0:T(1024)}, f32[1536]{0:T(1024)S(1)}, u32[]{:S(2)}) copy-start(f32[1536]{0:T(1024)S(1)} %get-tuple-element.46) | copy-start | bytes 18436
  140.9 3.7 copy-start.5
  183.8 2.2 copy-start.2
  186.0 2.2 copy-start.3
  540.4 99.1 %collective-permute-start = (f32[8960,768]{1,0:T(8,128)}, f32[8960,768]{1,0:T(8,128)}, u32[]{:S(2)}, u32[]{:S(2)}) collective-permute-start(f32[8960,768]{1,0:T(8,128)} %fusion.22), channel_id=1, source_target_pairs={{0,1},{1,0},{2,3},{3,2},{4,5},{5,4},{6,7},{7,6}} | collective-permute-start | bytes 82575368 | tf_op jit(solution)/shard_map/ppermute | solution.py:290
  845.8 54.4 %copy-start.4 = (bf16[3072,768]{1,0:T(8,128)(2,1)S(1)}, bf16[3072,768]{1,0:T(8,128)(2,1)}, u32[]{:S(2)}) copy-start(bf16[3072,768]{1,0:T(8,128)(2,1)} %copy-done.3) | copy-start | bytes 14155780
  899.8 51.8 %collective-permute-start.1 = (f32[768,8960]{1,0:T(8,128)}, f32[768,8960]{1,0:T(8,128)}, u32[]{:S(2)}, u32[]{:S(2)}) collective-permute-start(f32[768,8960]{1,0:T(8,128)} %fusion.32), channel_id=1, source_target_pairs={{0,1},{1,0},{2,3},{3,2},{4,5},{5,4},{6,7},{7,6}} | collective-permute-start | bytes 82575368 | tf_op jit(solution)/shard_map/ppermute | solution.py:308
  950.2 55.1 %collective-permute-start.2 = (f32[768,8960]{1,0:T(8,128)}, f32[768,8960]{1,0:T(8,128)}, u32[]{:S(2)}, u32[]{:S(2)}) collective-permute-start(f32[768,8960]{1,0:T(8,128)} %fusion.33), channel_id=1, source_target_pairs={{0,1},{1,0},{2,3},{3,2},{4,5},{5,4},{6,7},{7,6}} | collective-permute-start | bytes 82575368 | tf_op jit(solution)/shard_map/ppermute | solution.py:309
  951.5 583.5 %reduce-scatter.6.cloned.1.call-start = ((), (), s32[]{:S(2)}) async-start(), calls=%async_computation.10 | async-start | bytes 14155776 | tf_op jit(solution)/shard_map/reduce_scatter | solution.py:229
  1058.4 96.8 %copy-start.10 = (f32[1536]{0:T(1024)S(1)}, f32[1536]{0:T(1024)}, u32[]{:S(2)}) copy-start(f32[1536]{0:T(1024)} %copy-done.9) | copy-start | bytes 18436
  1058.4 96.8 %copy-start.11 = (f32[3072]{0:T(1024)S(1)}, f32[3072]{0:T(1024)}, u32[]{:S(2)}) copy-start(f32[3072]{0:T(1024)} %slice_reduce_fusion) | copy-start | bytes 36868
  1259.8 17.2 copy-start.6
  1273.5 3.5 copy-start.7
  1294.8 18.6 copy-start.1
  1313.5 109.7 %copy-start.14 = (f32[3072]{0:T(1024)S(1)}, f32[3072]{0:T(1024)}, u32[]{:S(2)}) copy-start(f32[3072]{0:T(1024)} %copy-done.13) | copy-start | bytes 36868
  1313.5 109.7 %copy-start.16 = (f32[1536]{0:T(1024)S(1)}, f32[1536]{0:T(1024)}, u32[]{:S(2)}) copy-start(f32[1536]{0:T(1024)} %copy-done.15) | copy-start | bytes 18436
  1450.7 156.8 %reduce-scatter.8.cloned.1.call-start = ((), (), s32[]{:S(2)}) async-start(), calls=%async_computation.11 | async-start | bytes 10616832 | tf_op jit(solution)/shard_map/reduce_scatter | solution.py:229
  1451.5 395.0 %reduce-scatter.10.cloned.1.call-start = ((), (), s32[]{:S(2)}) async-start(), calls=%async_computation.12 | async-start | bytes 34406400 | tf_op jit(solution)/shard_map/reduce_scatter | solution.py:229
  1452.2 633.0 %reduce-scatter.12.cloned.1.call-start = ((), (), s32[]{:S(2)}) async-start(), calls=%async_computation.13 | async-start | bytes 34406400 | tf_op jit(solution)/shard_map/reduce_scatter | solution.py:229
  1452.8 29.9 %copy-start.12 = (f32[1536]{0:T(1024)S(1)}, f32[1536]{0:T(1024)}, u32[]{:S(2)}) copy-start(f32[1536]{0:T(1024)} %get-tuple-element.43) | copy-start | bytes 18436
  1482.7 1.3 collective-permute-start.3
  1484.0 4.1 collective-permute-start.4
  1488.1 33.5 %collective-permute-start.5 = (f32[26,128]{1,0:T(8,128)S(1)}, f32[26,128]{1,0:T(8,128)S(1)}, u32[]{:S(2)}, u32[]{:S(2)}) collective-permute-start(f32[26,128]{1,0:T(8,128)S(1)} %fusion.67), channel_id=1, source_target_pairs={{0,4},{2,6},{4,0},{6,2},{1,5},{3,7},{5,1},{7,3}} | collective-permute-start | bytes 39944 | tf_op jit(solution)/shard_map/ppermute | solution.py:235
  1493.5 46.4 %collective-permute-start.6 = (f32[1120,768]{1,0:T(8,128)}, f32[1120,768]{1,0:T(8,128)}, u32[]{:S(2)}, u32[]{:S(2)}) collective-permute-start(f32[1120,768]{1,0:T(8,128)} %get-tuple-element.50), channel_id=1, source_target_pairs={{0,1},{1,0},{2,3},{3,2},{4,5},{5,4},{6,7},{7,6}} | collective-permute-start | bytes 10321928 | tf_op jit(solution)/shard_map/ppermute | solution.py:297
Sparse Core Ops, SparseCore 0:
  15.1 44.2 all-gather.5
  61.2 33.2 all-gather.7
  96.3 129.5 all-gather.9
  227.6 129.5 all-gather.11
  358.9 129.5 all-gather.13
  951.7 235.0 reduce-scatter.13
  1450.8 84.1 reduce-scatter.5
  1539.0 68.4 reduce-scatter.7
  1611.1 235.2 reduce-scatter.9
  1849.9 235.2 reduce-scatter.11

commit v2 on v1

--- a/solution.py
+++ b/solution.py
@@ -11,6 +11,7 @@
 
 RMS_EPS = 1e-6
 ROPE_THETA = 1000000.0
+LOG2_E = 1.4426950408889634
 F32 = jnp.float32
 BF16 = jnp.bfloat16
 
@@ -67,7 +68,7 @@
     tail = jnp.where(row <= col, tail, -1e30)
     scores = tail if key_len == q_len else jnp.concatenate([scores[:key_len - q_len], tail], axis=0)
     top = jnp.max(scores, axis=0, keepdims=True)
-    expo = jnp.exp((scores - top) * (head_dim ** -0.5))
+    expo = jnp.exp2((scores - top) * (head_dim ** -0.5 * LOG2_E))
     return expo * (1.0 / jnp.sum(expo, axis=0, keepdims=True))
 
 
@@ -108,13 +109,13 @@
             dv_acc[:stop, :] += matmul(probs.astype(BF16), d_out)
             d_probs = matmul_nt(v_seq[:stop], d_out)
             dot_row = jnp.sum(probs * d_probs, axis=0, keepdims=True)
-            d_scores = (probs * (d_probs - dot_row) * (head_dim ** -0.5)).astype(BF16)
+            d_scores = (probs * (d_probs - dot_row)).astype(BF16)
             dk_acc[:stop, :] += matmul(d_scores, q_blk)
             dq_tiles.append(matmul(k_t[:, :stop], d_scores).T)
-        d_proj, d_gain = head_backward(jnp.concatenate(dq_tiles, axis=0), q_unit, q_scale, qg_ref[...], cos_t, sin_t)
+        d_proj, d_gain = head_backward(jnp.concatenate(dq_tiles, axis=0) * (head_dim ** -0.5), q_unit, q_scale, qg_ref[...], cos_t, sin_t)
         dqkv_ref[:, lanes] = d_proj
         q_gain_sum += d_gain
-    d_proj, k_gain_sum = head_backward(dk_acc[...], k_unit, k_scale, kg_ref[...], cos_t, sin_t)
+    d_proj, k_gain_sum = head_backward(dk_acc[...] * (head_dim ** -0.5), k_unit, k_scale, kg_ref[...], cos_t, sin_t)
     dqkv_ref[:, base:base + head_dim] = d_proj
     dqkv_ref[:, base + head_dim:base + 2 * head_dim] = dv_acc[...].astype(BF16)
 
@@ -222,8 +223,8 @@
     out_specs = (sharded, sharded, sharded, sharded, P(), P()) + (sharded,) * 7
     swap = [(0, 1), (1, 0)]
 
-    def gather(shard):
-        return lax.all_gather(shard, both, axis=0, tiled=True)
+    def gather(shard, axes=both):
+        return lax.all_gather(shard, axes, axis=0, tiled=True)
 
     def scatter(part, axes):
         return lax.psum_scatter(part, axes, scatter_dimension=0, tiled=True)
@@ -261,9 +262,18 @@
         pieces.append(jnp.pad(jnp.stack([norm1_gain, norm2_gain], axis=1), ((0, 0), (0, head_dim - 2))))
         qkv_full = gather(jnp.concatenate(pieces, axis=1))
         wo_full = gather(w_o)
-        gate_full = gather(w_gate)
-        up_full = gather(w_up)
-        down_full = gather(w_down)
+        block = w_down.shape[0]
+        chunk = block * chips
+
+        def columns(weight, k):
+            return jnp.concatenate([weight[:, (2 * c + k) * block:(2 * c + k + 1) * block] for c in range(chips)], axis=1)
+
+        gate_w, up_w = [], []
+        for k in range(2):
+            gate_w.append(gather(columns(w_gate, k)))
+            up_w.append(gather(columns(w_up, k)))
+        down_full = gather(w_down, ("core", "chip"))
+        down_w = [down_full[:chunk], down_full[chunk:]]
         w_qkv = qkv_full[:, :qkv_width]
         gain1 = qkv_full[:, qkv_width].astype(F32)
         gain2 = qkv_full[:, qkv_width + 1].astype(F32)
@@ -281,39 +291,46 @@
         resid, r_wide, mlp_in, in_own, in_other = norm_split(core.reshape(1), hidden.reshape(tokens, width), attn_out, gain2.reshape(1, width), 256)
         resid_float = resid.astype(F32)
         r_scale = r_wide[:, :1]
-        gate_proj = matmul(mlp_in, gate_full).astype(BF16)
-        up_proj = matmul(mlp_in, up_full).astype(BF16)
-        mlp_act = (jax.nn.silu(gate_proj.astype(F32)) * up_proj.astype(F32)).astype(BF16)
+        gate_proj, up_proj, mlp_act = [], [], []
+        for k in range(2):
+            gate_proj.append(matmul(mlp_in, gate_w[k]).astype(BF16))
+            up_proj.append(matmul(mlp_in, up_w[k]).astype(BF16))
+            mlp_act.append((jax.nn.silu(gate_proj[k].astype(F32)) * up_proj[k].astype(F32)).astype(BF16))
 
         half = width // 2
         dy_own, dy_other = own(dy[:, :half], dy[:, half:]), own(dy[:, half:], dy[:, :half])
-        down_recv = lax.ppermute(matmul_tn(mlp_act, dy_other), "core", swap)
-        down_proj = matmul(mlp_act, down_full).astype(BF16)
-        layer_out = (resid_float + down_proj.astype(F32)).astype(BF16)
-        dy_own, layer_out = lax.optimization_barrier((dy_own, layer_out))
-        down_pair = (matmul_tn(mlp_act, dy_own) + down_recv) * inv_tokens
-        down_rows = scatter(down_pair, "chip")
-        drows = down_rows.shape[0] // 2
-        down_back = lax.ppermute(own(down_rows[drows:], down_rows[:drows]), "core", swap)
-        down_mine = own(down_rows[:drows], down_rows[drows:])
+        down_recv = [lax.ppermute(matmul_tn(mlp_act[k], dy_other), "core", swap) for k in range(2)]
+        dy_own, _ = lax.optimization_barrier((dy_own, mlp_act[1]))
+        down_pair = [(matmul_tn(mlp_act[k], dy_own) + down_recv[k]) * inv_tokens for k in range(2)]
+        down_rows = [scatter(down_pair[k], "chip") for k in range(2)]
+        down_back = lax.ppermute(own(down_rows[1], down_rows[0]), "core", swap)
+        down_mine = own(down_rows[0], down_rows[1])
         g_down = own(jnp.concatenate([down_mine, down_back], axis=1), jnp.concatenate([down_back, down_mine], axis=1))
 
-        dy_late, layer_out, _ = lax.optimization_barrier((dy, layer_out, down_pair))
-        d_mlp_act = matmul_nt(dy_late, down_full)
-        gate_float = gate_proj.astype(F32)
-        gate_sig = jax.nn.sigmoid(gate_float)
-        d_up = (d_mlp_act * gate_float * gate_sig).astype(BF16)
-        d_gate = (d_mlp_act * up_proj.astype(F32) * gate_sig * (1.0 + gate_float * (1.0 - gate_sig))).astype(BF16)
-
-        gate_recv = lax.ppermute(matmul_tn(in_other, d_gate), "core", swap)
-        up_recv = lax.ppermute(matmul_tn(in_other, d_up), "core", swap)
-        gate_pair = (matmul_tn(in_own, d_gate) + gate_recv) * inv_tokens
-        up_pair = (matmul_tn(in_own, d_up) + up_recv) * inv_tokens
-        g_gate = scatter(gate_pair, "chip")
-        g_up = scatter(up_pair, "chip")
-        d_gate, d_up, _, _ = lax.optimization_barrier((d_gate, d_up, gate_pair, up_pair))
-
-        d_mlp_in = matmul_nt(d_gate, gate_full) + matmul_nt(d_up, up_full)
+        held = tuple(down_pair)
+        dy_late = dy
+        d_gate, d_up, gate_rows, up_rows = [], [], [], []
+        for k in range(2):
+            dy_late = lax.optimization_barrier((dy_late,) + held)[0]
+            d_mlp_act = matmul_nt(dy_late, down_w[k])
+            gate_float = gate_proj[k].astype(F32)
+            gate_sig = jax.nn.sigmoid(gate_float)
+            d_up.append((d_mlp_act * gate_float * gate_sig).astype(BF16))
+            d_gate.append((d_mlp_act * up_proj[k].astype(F32) * gate_sig * (1.0 + gate_float * (1.0 - gate_sig))).astype(BF16))
+            gate_recv = lax.ppermute(matmul_tn(in_other, d_gate[k]), "core", swap)
+            up_recv = lax.ppermute(matmul_tn(in_other, d_up[k]), "core", swap)
+            gate_pair = (matmul_tn(in_own, d_gate[k]) + gate_recv) * inv_tokens
+            up_pair = (matmul_tn(in_own, d_up[k]) + up_recv) * inv_tokens
+            gate_rows.append(scatter(gate_pair, "chip"))
+            up_rows.append(scatter(up_pair, "chip"))
+            held = (gate_pair, up_pair)
+
+        def interleave(parts):
+            return jnp.concatenate([parts[i % 2][:, (i // 2) * block:(i // 2 + 1) * block] for i in range(2 * chips)], axis=1)
+
+        g_gate, g_up = interleave(gate_rows), interleave(up_rows)
+        late = lax.optimization_barrier((d_gate[0], d_up[0], d_gate[1], d_up[1]) + held)
+        d_mlp_in = matmul_nt(late[0], gate_w[0]) + matmul_nt(late[1], up_w[0]) + matmul_nt(late[2], gate_w[1]) + matmul_nt(late[3], up_w[1])
         r_unit = resid_float * r_scale
         grad_norm2 = jnp.sum(d_mlp_in * r_unit, axis=0)
         d_resid = dy.astype(F32) + norm_backward(d_mlp_in * gain2, r_unit, r_scale)
@@ -323,12 +340,17 @@
         d_resid_bf, _ = lax.optimization_barrier((d_resid_bf, wo_part))
         d_ctx = matmul_nt(d_resid_bf, wo_full).astype(BF16)
         d_qkv, gain_sums = attention_backward(qkv, cos_t, sin_t, q_gain, k_gain, d_ctx, batch, group, kv_heads, head_dim, q_tile)
-        g_qkv = scatter(matmul_tn(normed, d_qkv) * inv_tokens, both)
+        qkv_part = matmul_tn(normed, d_qkv) * inv_tokens
+        g_qkv = scatter(qkv_part, both)
 
         d_normed = matmul_nt(d_qkv, w_qkv)
         x_unit = x_float * x_scale
         grad_norm1 = jnp.sum(d_normed * x_unit, axis=0)
         d_hidden = (d_resid + norm_backward(d_normed * gain1, x_unit, x_scale)).astype(BF16)
+
+        act0, act1, d_hidden, _ = lax.optimization_barrier((mlp_act[0], mlp_act[1], d_hidden, qkv_part))
+        down_proj = (matmul(act0, down_w[0]) + matmul(act1, down_w[1])).astype(BF16)
+        layer_out = (resid_float + down_proj.astype(F32)).astype(BF16)
 
         small = jnp.concatenate([grad_norm1, grad_norm2, gain_sums[0], gain_sums[1]]) * inv_tokens
         small = sum_all(small.reshape(-1, 128)).reshape(-1)

time: 2100 us -> 1820 us (0.87)
  waiting for transfers between devices: 652 us -> 218 us
  matrix products: 1140 us -> 1230 us
  local copies, waits for them, and re-layouts: 25.2 us -> 88 us
    reduce_scatter x5 -> x8, waiting for transfers between devices: 549 us -> 180 us  [scatter(): return lax.psum_scatter(part, axes, scatter_dimension=0, tiled=True)]
    all_gather x5 -> x7, waiting for transfers between devices: 95.8 us -> 2.89 us  [gather(): return lax.all_gather(shard, axes, axis=0, tiled=True)]
    dot_general x8 -> x14, matrix products: 364 us -> 417 us  [matmul_tn(): lax.dot_general(left_op, right_op, (((0,), (0,)), ((), ())), preferred_el...]
    concatenate x0 -> x6, local copies, waits for them, and re-layouts: none -> 34.1 us  [the longest x4 17.1 us: columns(): jnp.concatenate([weight[:, (2 * c + k) * block:(2 * c + k + 1) * block] f...]
    ppermute x4 -> x7, waiting for transfers between devices: 0.01 us -> 32.2 us  [the longest x2 22.9 us: device_step(): lax.ppermute(matmul_tn(mlp_act[k], dy_other), 'core', swap)]
    dot_general x5 -> x8, matrix products: 402 us -> 430 us  [matmul_nt(): lax.dot_general(left_op, right_op, (((1,), (1,)), ((), ())), preferred_el...]
    slice x0 -> x6, local copies, waits for them, and re-layouts: none -> 24.5 us  [the longest x4 16.4 us: interleave(): parts[i % 2][:, i // 2 * block:(i // 2 + 1) * block]]
    dot_general x5 -> x8, matrix products: 370 us -> 380 us  [matmul(): return jnp.dot(left_op, right_op, preferred_element_type=F32)]
  transfers between devices with their start and end apart: 17 -> 25, of which waited for: 9 -> 6; matrix products, arithmetic and copies ran while one was open for 46% -> 76% of each run, Pallas kernels for 9% -> 10%
where the time goes in v2:
time: 1820 us; the launch traced here: 1810 us
  matrix products  1230 us (68%)
  waiting for transfers between devices  218 us (12%)
  Pallas kernels  177 us (10%)
  local copies, waits for them, and re-layouts  88 us (5%)
  other arithmetic  79.4 us (4%)
    dot_general x8, matrix products, matmul_nt(): lax.dot_general(left_op, right_op, (((1,), (1,)), ((), ())), preferred_el...  430 us
    dot_general x14, matrix products, matmul_tn(): lax.dot_general(left_op, right_op, (((0,), (0,)), ((), ())), preferred_el...  417 us
    dot_general x8, matrix products, matmul(): return jnp.dot(left_op, right_op, preferred_element_type=F32)  380 us
    reduce_scatter x8, waiting for transfers between devices, scatter(): return lax.psum_scatter(part, axes, scatter_dimension=0, tiled=True)  180 us
    pallas_call x1, Pallas kernels, attention_backward(): pl.pallas_call(functools.partial(attention_backward_kernel, group, head_d...  107 us
    pallas_call x1, Pallas kernels, attention_forward(): pl.pallas_call(functools.partial(attention_forward_kernel, group, head_di...  52 us
  transfers between devices with their start and end apart: 25, of which 6 were waited for; matrix products, arithmetic and copies ran while one was open for 76% of the time, Pallas kernels for 10%

profile of v2, /device:TPU:0, one launch (start us, length us, event | category | flops | bytes accessed | tf_op | source)
XLA Modules:
  0.0 1811.9 jit_solution(6435630912670030878)
XLA Ops:
  19.6 5.1 fusion.50
  24.7 4.3 concatenate.48
  29.0 3.1 fusion.51
  32.1 4.2 concatenate.49
  36.4 4.2 concatenate.50
  40.7 4.4 concatenate.51
  46.3 5.7 multiply_reduce_fusion.2
  52.1 5.8 fusion.43
  57.9 6.5 broadcast_select_fusion.1
  65.3 2.1 convert_reduce_fusion
  68.0 26.4 %convolution_convert_fusion.6.qkv_ref = bf16[3072,2048]{1,0:T(8,128)(2,1)} fusion(bf16[1536,2176]{1,0:T(8,128)(2,1)} %all-gather.8.cloned.1.call-done, bf16[3072,1536]{1,0:T(8,128)(2,1)} %bitcast.100, f32[1536]{0:T(1024)S(1)} %get-tuple-element.54, f32[3072]{0:T(1024)S(1)} %rsqrt.12), kind=kOutput, calls=%fused_computation.70 | convolution fusion | flops 19352518656 | bytes 28329984 | tf_op jit(solution)/shard_map/dot_general | solution.py:28
  94.4 52.0 %attn_fwd.1 = bf16[3072,1536]{1,0:T(8,128)(2,1)S(1)} custom-call(bf16[3072,2048]{1,0:T(8,128)(2,1)} %convolution_convert_fusion.6.qkv_ref, f32[3072,128]{1,0:T(8,128)S(1)} %get-tuple-element.114.cos_ref, f32[3072,128]{1,0:T(8,128)S(1)} %get-tuple-element.115.sin_ref, f32[1,128]{1,0:T(1,128)S(1)} %get-tuple-element.117.qg_ref, ...), custom_call_target="tpu_custom_call" | custom-call | flops 7247757312 | bytes 25165824 | tf_op jit(solution)/shard_map/attn_fwd/pallas_call | solution.py:188
  146.5 3.7 copy-done.6
  150.2 20.3 %convolution_convert_fusion.5.attn_ref = bf16[3072,1536]{1,0:T(8,128)(2,1)} fusion(bf16[3072,1536]{1,0:T(8,128)(2,1)} %copy-done.6, bf16[1536,1536]{1,0:T(8,128)(2,1)} %all-gather.10.cloned.1.call-done), kind=kOutput, calls=%fused_computation.69 | convolution fusion | flops 14500233216 | bytes 23592960 | tf_op jit(solution)/shard_map/dot_general | solution.py:28
  170.5 18.3 %norm_split.1 = (bf16[3072,1536]{1,0:T(8,128)(2,1)}, f32[3072,128]{1,0:T(8,128)S(1)}, bf16[3072,1536]{1,0:T(8,128)(2,1)}, bf16[3072,768]{1,0:T(8,128)(2,1)S(1)}, bf16[3072,768]{1,0:T(8,128)(2,1)S(1)}) custom-call(s32[1]{0:T(128)} %bitcast.flag_ref, bf16[3072,1536]{1,0:T(8,128)(2,1)} %bitcast.101, bf16[3072,1536]{1,0:T(8,128)(2,1)} %convolution_convert_fusion.5.attn_ref, ...), custom_call_target="tpu_custom_call" | custom-call | flops 94371840 | bytes 47185920 | tf_op jit(solution)/shard_map/norm_split/pallas_call | solution.py:155
  188.8 2.2 copy-done.2
  191.0 2.2 copy-done.3
  193.2 52.0 %convolution_convert_fusion.3 = bf16[3072,4480]{1,0:T(8,128)(2,1)} fusion(bf16[3072,1536]{1,0:T(8,128)(2,1)} %get-tuple-element.32, bf16[1536,4480]{1,0:T(8,128)(2,1)} %all-gather.12.cloned.1.call-done), kind=kOutput, calls=%fused_computation.35 | convolution fusion | flops 42292346880 | bytes 50724864 | tf_op jit(solution)/shard_map/dot_general | solution.py:28
  245.2 60.1 %fusion = (bf16[3072,4480]{1,0:T(8,128)(2,1)}, bf16[3072,4480]{1,0:T(8,128)(2,1)}) fusion(bf16[3072,4480]{1,0:T(8,128)(2,1)} %convolution_convert_fusion.3, bf16[3072,1536]{1,0:T(8,128)(2,1)} %get-tuple-element.32, bf16[1536,4480]{1,0:T(8,128)(2,1)} %all-gather.14.cloned.1.call-done), kind=kOutput, calls=%fused_computation.12 | convolution fusion | flops 42402447360 | bytes 105775104 | tf_op jit(solution)/shard_map/dot_general | solution.py:28
  305.2 30.1 %fusion.42 = f32[4480,768]{1,0:T(8,128)} fusion(bf16[3072,4480]{1,0:T(8,128)(2,1)} %get-tuple-element.45, pred[]{:T(512)S(6)} %eq.3, bf16[3072,1536]{1,0:T(8,128)(2,1)} %bitcast.94), kind=kOutput, calls=%fused_computation.90 | convolution fusion | flops 21141651456 | bytes 50724864 | tf_op jit(solution)/shard_map/dot_general | solution.py:32
  336.2 51.9 %convolution_convert_fusion.1 = bf16[3072,4480]{1,0:T(8,128)(2,1)} fusion(bf16[3072,1536]{1,0:T(8,128)(2,1)} %get-tuple-element.32, bf16[1536,4480]{1,0:T(8,128)(2,1)} %all-gather.16.cloned.1.call-done), kind=kOutput, calls=%fused_computation.33 | convolution fusion | flops 42292346880 | bytes 50724864 | tf_op jit(solution)/shard_map/dot_general | solution.py:28
  388.1 2.8 all-gather.18.cloned.1.call-done
  391.0 60.6 %fusion.4 = (bf16[3072,4480]{1,0:T(8,128)(2,1)}, bf16[3072,4480]{1,0:T(8,128)(2,1)}) fusion(bf16[3072,4480]{1,0:T(8,128)(2,1)} %convolution_convert_fusion.1, bf16[3072,1536]{1,0:T(8,128)(2,1)} %get-tuple-element.32, bf16[1536,4480]{1,0:T(8,128)(2,1)} %all-gather.18.cloned.1.call-done), kind=kOutput, calls=%fused_computation.16 | convolution fusion | flops 42402447360 | bytes 105775104 | tf_op jit(solution)/shard_map/dot_general | solution.py:28
  451.6 30.8 %add_multiply_fusion.5 = f32[4480,768]{1,0:T(8,128)} fusion(f32[4480,768]{1,0:T(8,128)} %collective-permute-done, bf16[3072,4480]{1,0:T(8,128)(2,1)} %get-tuple-element.45, bf16[3072,768]{1,0:T(8,128)(2,1)} %broadcast_select_fusion.1), kind=kOutput, calls=%fused_computation.60 | convolution fusion | flops 21146173440 | bytes 59768832 | tf_op jit(solution)/shard_map/dot_general | solution.py:32
  482.4 30.6 %fusion.41 = f32[4480,768]{1,0:T(8,128)} fusion(bf16[3072,4480]{1,0:T(8,128)(2,1)} %get-tuple-element.46, pred[]{:T(512)S(6)} %eq.3, bf16[3072,1536]{1,0:T(8,128)(2,1)} %bitcast.95), kind=kOutput, calls=%fused_computation.89 | convolution fusion | flops 21141651456 | bytes 50724864 | tf_op jit(solution)/shard_map/dot_general | solution.py:32
  513.0 22.9 %collective-permute-done.1 = f32[4480,768]{1,0:T(8,128)S(1)} collective-permute-done((f32[4480,768]{1,0:T(8,128)}, f32[4480,768]{1,0:T(8,128)S(1)}, u32[]{:S(2)}, u32[]{:S(2)}) %collective-permute-start.1) | collective-permute-done | bytes 13762592 | tf_op jit(solution)/shard_map/ppermute | solution.py:302
  535.9 28.9 %add_multiply_fusion.4 = f32[4480,768]{1,0:T(8,128)} fusion(f32[4480,768]{1,0:T(8,128)S(1)} %collective-permute-done.1, bf16[3072,4480]{1,0:T(8,128)(2,1)} %get-tuple-element.46, bf16[3072,768]{1,0:T(8,128)(2,1)} %broadcast_select_fusion.1), kind=kOutput, calls=%fused_computation.59 | convolution fusion | flops 21146173440 | bytes 59768832 | tf_op jit(solution)/shard_map/dot_general | solution.py:32
  564.9 82.8 %fusion.13 = (bf16[3072,4480]{1,0:T(8,128)(2,1)}, bf16[3072,4480]{1,0:T(8,128)(2,1)}) fusion(bf16[3072,4480]{1,0:T(8,128)(2,1)} %convolution_convert_fusion.3, bf16[3072,4480]{1,0:T(8,128)(2,1)} %get-tuple-element.109, bf16[3072,1536]{1,0:T(8,128)(2,1)} %bitcast.96, bf16[8960,1536]{1,0:T(8,128)(2,1)} %all-gather.20.cloned.1.call-done), kind=kOutput, calls=%fused_computation.25 | convolution fusion | flops 42485022720 | bytes 133300224 | tf_op jit(solution)/shard_map/dot_general | solution.py:36
  647.7 32.7 %fusion.54 = f32[768,4480]{1,0:T(8,128)} fusion(bf16[3072,768]{1,0:T(8,128)(2,1)} %copy-done.3, bf16[3072,4480]{1,0:T(8,128)(2,1)} %get-tuple-element.39), kind=kOutput, calls=%fused_computation.125 | convolution fusion | flops 21139292160 | bytes 46006272 | tf_op jit(solution)/shard_map/dot_general | solution.py:32
  680.9 29.4 %fusion.55 = f32[768,4480]{1,0:T(8,128)} fusion(bf16[3072,768]{1,0:T(8,128)(2,1)S(1)} %copy-done.4, bf16[3072,4480]{1,0:T(8,128)(2,1)} %get-tuple-element.40), kind=kOutput, calls=%fused_computation.126 | convolution fusion | flops 21139292160 | bytes 46006272 | tf_op jit(solution)/shard_map/dot_general | solution.py:32
  710.4 30.7 %add_multiply_fusion.3 = f32[768,4480]{1,0:T(8,128)} fusion(f32[768,4480]{1,0:T(8,128)} %collective-permute-done.2, bf16[3072,768]{1,0:T(8,128)(2,1)S(1)} %bitcast.92, bf16[3072,4480]{1,0:T(8,128)(2,1)} %get-tuple-element.39), kind=kOutput, calls=%fused_computation.58 | convolution fusion | flops 21146173440 | bytes 59768832 | tf_op jit(solution)/shard_map/dot_general | solution.py:32
  741.2 31.7 %add_multiply_fusion.2 = f32[768,4480]{1,0:T(8,128)} fusion(f32[768,4480]{1,0:T(8,128)} %collective-permute-done.3, bf16[3072,768]{1,0:T(8,128)(2,1)} %copy-done.2, bf16[3072,4480]{1,0:T(8,128)(2,1)} %get-tuple-element.40), kind=kOutput, calls=%fused_computation.57 | convolution fusion | flops 21146173440 | bytes 59768832 | tf_op jit(solution)/shard_map/dot_general | solution.py:32
  772.8 82.2 %fusion.19 = (bf16[3072,4480]{1,0:T(8,128)(2,1)}, bf16[3072,4480]{1,0:T(8,128)(2,1)}) fusion(bf16[3072,4480]{1,0:T(8,128)(2,1)} %convolution_convert_fusion.1, bf16[3072,4480]{1,0:T(8,128)(2,1)} %get-tuple-element.111, bf16[3072,1536]{1,0:T(8,128)(2,1)} %bitcast.97, bf16[8960,1536]{1,0:T(8,128)(2,1)} %all-gather.20.cloned.1.call-done), kind=kOutput, calls=%fused_computation.31 | convolution fusion | flops 42485022720 | bytes 133300224 | tf_op jit(solution)/shard_map/dot_general | solution.py:36
  855.0 32.8 %fusion.56 = f32[768,4480]{1,0:T(8,128)} fusion(bf16[3072,768]{1,0:T(8,128)(2,1)} %copy-done.3, bf16[3072,4480]{1,0:T(8,128)(2,1)} %get-tuple-element.41), kind=kOutput, calls=%fused_computation.127 | convolution fusion | flops 21139292160 | bytes 46006272 | tf_op jit(solution)/shard_map/dot_general | solution.py:32
  888.5 29.7 %fusion.57 = f32[768,4480]{1,0:T(8,128)} fusion(bf16[3072,768]{1,0:T(8,128)(2,1)S(1)} %copy-done.5, bf16[3072,4480]{1,0:T(8,128)(2,1)} %get-tuple-element.42), kind=kOutput, calls=%fused_computation.128 | convolution fusion | flops 21139292160 | bytes 46006272 | tf_op jit(solution)/shard_map/dot_general | solution.py:32
  919.3 32.6 %add_multiply_fusion.1 = f32[768,4480]{1,0:T(8,128)} fusion(f32[768,4480]{1,0:T(8,128)} %collective-permute-done.4, bf16[3072,768]{1,0:T(8,128)(2,1)} %copy-done.2, bf16[3072,4480]{1,0:T(8,128)(2,1)} %get-tuple-element.41), kind=kOutput, calls=%fused_computation.56 | convolution fusion | flops 21146173440 | bytes 59768832 | tf_op jit(solution)/shard_map/dot_general | solution.py:32
  951.9 32.0 %add_multiply_fusion = f32[768,4480]{1,0:T(8,128)} fusion(f32[768,4480]{1,0:T(8,128)} %collective-permute-done.5, bf16[3072,768]{1,0:T(8,128)(2,1)} %copy-done.2, bf16[3072,4480]{1,0:T(8,128)(2,1)} %get-tuple-element.42), kind=kOutput, calls=%fused_computation.55 | convolution fusion | flops 21146173440 | bytes 59768832 | tf_op jit(solution)/shard_map/dot_general | solution.py:32
  983.9 53.0 %fusion.58 = f32[3072,1536]{1,0:T(8,128)} fusion(bf16[3072,4480]{1,0:T(8,128)(2,1)} %get-tuple-element.39, bf16[1536,4480]{1,0:T(8,128)(2,1)} %all-gather.12.cloned.1.call-done), kind=kOutput, calls=%fused_computation.129 | convolution fusion | flops 42278584320 | bytes 60162048 | tf_op jit(solution)/shard_map/dot_general | solution.py:36
  1037.0 53.5 %fusion.59 = f32[3072,1536]{1,0:T(8,128)} fusion(bf16[3072,4480]{1,0:T(8,128)(2,1)} %get-tuple-element.40, bf16[1536,4480]{1,0:T(8,128)(2,1)} %all-gather.14.cloned.1.call-done), kind=kOutput, calls=%fused_computation.130 | convolution fusion | flops 42278584320 | bytes 60162048 | tf_op jit(solution)/shard_map/dot_general | solution.py:36
  1090.4 53.0 %fusion.60 = f32[3072,1536]{1,0:T(8,128)} fusion(bf16[3072,4480]{1,0:T(8,128)(2,1)} %get-tuple-element.41, bf16[1536,4480]{1,0:T(8,128)(2,1)} %all-gather.16.cloned.1.call-done), kind=kOutput, calls=%fused_computation.131 | convolution fusion | flops 42278584320 | bytes 60162048 | tf_op jit(solution)/shard_map/dot_general | solution.py:36
  1143.5 58.8 %fusion.27 = (f32[1536]{0:T(1024)}, f32[3072]{0:T(1024)S(1)}, f32[3072,1536]{1,0:T(8,128)}) fusion(bf16[3072,1536]{1,0:T(8,128)(2,1)} %get-tuple-element.31, f32[3072]{0:T(1024)S(1)} %copy-done.12, f32[1536]{0:T(1024)S(1)} %copy-done.11, bf16[3072,4480]{1,0:T(8,128)(2,1)} %get-tuple-element.42, bf16[1536,4480]{1,0:T(8,128)(2,1)} %all-gather.18.cloned.1.call-done, ...), kind=kOutput, calls=%fused_computation.45 | convolution fusion | flops 42325766144 | bytes 126259200 | tf_op jit(solution)/shard_map/dot_general | solution.py:36
  1202.3 13.8 fusion.45
  1216.1 3.7 copy-done.8
  1219.8 17.9 convolution_multiply_fusion.1
  1237.8 18.6 %convolution_convert_fusion.4.dctx_ref = bf16[3072,1536]{1,0:T(8,128)(2,1)S(1)} fusion(bf16[3072,1536]{1,0:T(8,128)(2,1)} %copy-done.8, bf16[1536,1536]{1,0:T(8,128)(2,1)} %all-gather.10.cloned.1.call-done), kind=kOutput, calls=%fused_computation.68 | convolution fusion | flops 14500233216 | bytes 23592960 | tf_op jit(solution)/shard_map/dot_general | solution.py:36
  1256.4 106.6 %attn_bwd.1 = (bf16[3072,2048]{1,0:T(8,128)(2,1)}, f32[8,128]{1,0:T(8,128)S(1)}) custom-call(bf16[3072,2048]{1,0:T(8,128)(2,1)} %convolution_convert_fusion.6.qkv_ref, f32[3072,128]{1,0:T(8,128)S(1)} %copy-done.1, f32[3072,128]{1,0:T(8,128)S(1)} %get-tuple-element.115.sin_ref, f32[1,128]{1,0:T(1,128)S(1)} %get-tuple-element.117.qg_ref, ...), custom_call_target="tpu_custom_call" | custom-call | flops 19327352832 | bytes 50331648 | tf_op jit(solution)/shard_map/attn_bwd/pallas_call | solution.py:204
  1363.1 27.5 %convolution_multiply_fusion = f32[1536,2048]{1,0:T(8,128)} fusion(bf16[3072,2048]{1,0:T(8,128)(2,1)} %get-tuple-element.44, bf16[3072,1536]{1,0:T(8,128)(2,1)} %bitcast.102, f32[1536]{0:T(1024)S(1)} %copy-done.17, f32[3072]{0:T(1024)S(1)} %copy-done.15), kind=kOutput, calls=%fused_computation.71 | convolution fusion | flops 19349372928 | bytes 34621440 | tf_op jit(solution)/shard_map/dot_general | solution.py:32
  1392.1 9.0 broadcast_select_fusion.3
  1401.7 9.3 collective-permute-done.9
  1411.0 9.1 maximum_select_fusion
  1420.2 28.4 %multiply_reduce_fusion = (f32[1536]{0:T(1024)S(1)}, f32[3072]{0:T(1024)S(1)}, f32[3072,1536]{1,0:T(8,128)}) fusion(f32[3072]{0:T(1024)S(1)} %copy-done.15, bf16[6,512,1536]{2,1,0:T(8,128)(2,1)} %param.14, f32[1536]{0:T(1024)S(1)} %copy-done.17, bf16[3072,2048]{1,0:T(8,128)(2,1)} %get-tuple-element.44, bf16[1536,2176]{1,0:T(8,128)(2,1)} %all-gather.8.cloned.1.call-done), kind=kOutput, calls=%fused_computation.47 | convolution fusion | flops 19360378880 | bytes 47222784 | tf_op jit(solution)/shard_map/dot_general | solution.py:36
  1449.2 23.9 %add_convert_fusion.1 = bf16[3072,1536]{1,0:T(8,128)(2,1)} fusion(f32[3072,1536]{1,0:T(8,128)} %get-tuple-element.113, f32[3072]{0:T(1024)S(1)} %broadcast_multiply_fusion, f32[1536]{0:T(1024)S(1)} %copy-done.17, f32[3072]{0:T(1024)S(1)} %copy-done.15, bf16[6,512,1536]{2,1,0:T(8,128)(2,1)} %param.14, f32[3072]{0:T(1024)S(1)} %broadcast_multiply_fusion.1, ...), kind=kLoop, calls=%fused_computation.49 | loop fusion | flops 75497472 | bytes 75558912 | tf_op jit(solution)/shard_map/convert_element_type | solution.py:349
  1473.1 2.6 collective-permute-start.7
  1475.7 53.7 %fusion.32 = f32[3072,1536]{1,0:T(8,128)} fusion(bf16[3072,4480]{1,0:T(8,128)(2,1)} %get-tuple-element.45, bf16[8960,1536]{1,0:T(8,128)(2,1)} %all-gather.20.cloned.1.call-done), kind=kOutput, calls=%fused_computation.64 | convolution fusion | flops 42278584320 | bytes 60162048 | tf_op jit(solution)/shard_map/dot_general | solution.py:28
  1530.8 54.6 %fusion.28 = bf16[3072,1536]{1,0:T(8,128)(2,1)} fusion(bf16[3072,1536]{1,0:T(8,128)(2,1)} %get-tuple-element.31, f32[3072,1536]{1,0:T(8,128)} %fusion.32, bf16[3072,4480]{1,0:T(8,128)(2,1)} %get-tuple-element.46, bf16[8960,1536]{1,0:T(8,128)(2,1)} %all-gather.20.cloned.1.call-done), kind=kOutput, calls=%fused_computation.46 | convolution fusion | flops 42306895872 | bytes 79036416 | tf_op jit(solution)/shard_map/dot_general | solution.py:28
  1587.3 4.6 fusion.49
  1591.8 2.8 fusion.47
  1599.6 5.7 reduce-scatter.15.cloned.1.call-done
  1605.2 4.5 fusion.48
  1609.7 8.7 concatenate.56
  1618.5 114.4 %reduce-scatter.19.cloned.1.call-done = f32[192,4480]{1,0:T(8,128)} async-done(((f32[768,4480]{1,0:T(8,128)}), f32[192,4480]{1,0:T(8,128)}) %reduce-scatter.19.cloned.1.call-update) | async-done | bytes 3440656 | tf_op jit(solution)/shard_map/reduce_scatter | solution.py:230
  1732.9 4.5 fusion.46
  1737.4 8.3 concatenate.57
  1745.7 59.5 %reduce-scatter.11.cloned.1.call-done = f32[192,1536]{1,0:T(8,128)} async-done(((f32[1536,1536]{1,0:T(8,128)}), f32[192,1536]{1,0:T(8,128)}) %reduce-scatter.11.cloned.1.call-update) | async-done | bytes 1179664 | tf_op jit(solution)/shard_map/reduce_scatter | solution.py:230
  (144 shorter events, 29.4 us)
Async XLA Ops:
  7.2 21.9 %copy-start.9 = (bf16[192,8960]{1,0:T(8,128)(2,1)S(1)}, bf16[192,8960]{1,0:T(8,128)(2,1)}, u32[]{:S(2)}) copy-start(bf16[192,8960]{1,0:T(8,128)(2,1)} %param.26) | copy-start | bytes 10321924
  7.2 58.1 %all-gather.8.cloned.1.call-start = ((), (), s32[]{:S(2)}) async-start(), calls=%async_computation.8 | async-start | bytes 7520256 | tf_op jit(solution)/shard_map/all_gather | solution.py:227
  18.8 131.4 %all-gather.10.cloned.1.call-start = ((), (), s32[]{:S(2)}) async-start(), calls=%async_computation.9 | async-start | bytes 5308416 | tf_op jit(solution)/shard_map/all_gather | solution.py:227
  19.5 173.7 %all-gather.12.cloned.1.call-start = ((), (), s32[]{:S(2)}) async-start(), calls=%async_computation.10 | async-start | bytes 15482880 | tf_op jit(solution)/shard_map/all_gather | solution.py:227
  29.0 17.3 copy-start.18
  29.0 216.2 %all-gather.14.cloned.1.call-start = ((), (), s32[]{:S(2)}) async-start(), calls=%async_computation.11 | async-start | bytes 15482880 | tf_op jit(solution)/shard_map/all_gather | solution.py:227
  32.1 19.9 %copy-start.19 = (bf16[128]{0:T(256)(128)(2,1)S(1)}, bf16[128]{0:T(256)(128)(2,1)}, u32[]{:S(2)}) copy-start(bf16[128]{0:T(256)(128)(2,1)} %param.20) | copy-start | bytes 772
  32.1 19.9 %copy-start.20 = (bf16[128]{0:T(256)(128)(2,1)S(1)}, bf16[128]{0:T(256)(128)(2,1)}, u32[]{:S(2)}) copy-start(bf16[128]{0:T(256)(128)(2,1)} %param.19) | copy-start | bytes 772
  36.4 299.8 %all-gather.16.cloned.1.call-start = ((), (), s32[]{:S(2)}) async-start(), calls=%async_computation.12 | async-start | bytes 15482880 | tf_op jit(solution)/shard_map/all_gather | solution.py:227
  40.6 350.3 %all-gather.18.cloned.1.call-start = ((), (), s32[]{:S(2)}) async-start(), calls=%async_computation.13 | async-start | bytes 15482880 | tf_op jit(solution)/shard_map/all_gather | solution.py:227
  45.1 519.8 %all-gather.20.cloned.1.call-start = ((), (), s32[]{:S(2)}) async-start(), calls=%async_computation.14 | async-start | bytes 30965760 | tf_op jit(solution)/shard_map/all_gather | solution.py:227
  45.9 1346.2 %reduce-scatter.21.cloned.1.call-start = ((), (), s32[]{:S(2)}) async-start(), calls=%async_computation.21 | async-start | bytes 17203200 | tf_op jit(solution)/shard_map/reduce_scatter | solution.py:230
  52.0 16.0 copy-start.14
  65.3 29.2 %copy-start = (f32[3072,128]{1,0:T(8,128)}, f32[3072,128]{1,0:T(8,128)S(1)}, u32[]{:S(2)}) copy-start(f32[3072,128]{1,0:T(8,128)S(1)} %get-tuple-element.114.cos_ref) | copy-start | bytes 4718596
  67.4 0.6 copy-start.10
  67.4 27.0 %copy-start.16 = (f32[1536]{0:T(1024)}, f32[1536]{0:T(1024)S(1)}, u32[]{:S(2)}) copy-start(f32[1536]{0:T(1024)S(1)} %get-tuple-element.54) | copy-start | bytes 18436
  146.5 3.7 copy-start.6
  188.8 2.2 copy-start.2
  191.0 2.2 copy-start.3
  335.3 116.3 %collective-permute-start = (f32[4480,768]{1,0:T(8,128)}, f32[4480,768]{1,0:T(8,128)}, u32[]{:S(2)}, u32[]{:S(2)}) collective-permute-start(f32[4480,768]{1,0:T(8,128)} %fusion.42), channel_id=1, source_target_pairs={{0,1},{1,0},{2,3},{3,2},{4,5},{5,4},{6,7},{7,6}} | collective-permute-start | bytes 41287688 | tf_op jit(solution)/shard_map/ppermute | solution.py:302
  482.4 909.7 %reduce-scatter.23.cloned.1.call-start = ((), (), s32[]{:S(2)}) async-start(), calls=%async_computation.22 | async-start | bytes 17203200 | tf_op jit(solution)/shard_map/reduce_scatter | solution.py:230
  513.0 22.9 %collective-permute-start.1 = (f32[4480,768]{1,0:T(8,128)}, f32[4480,768]{1,0:T(8,128)S(1)}, u32[]{:S(2)}, u32[]{:S(2)}) collective-permute-start(f32[4480,768]{1,0:T(8,128)} %fusion.41), channel_id=1, source_target_pairs={{0,1},{1,0},{2,3},{3,2},{4,5},{5,4},{6,7},{7,6}} | collective-permute-start | bytes 41287688 | tf_op jit(solution)/shard_map/ppermute | solution.py:302
  564.9 1022.4 %reduce-scatter.13.cloned.1.call-start = ((), (), s32[]{:S(2)}) async-start(), calls=%async_computation.17 | async-start | bytes 17203200 | tf_op jit(solution)/shard_map/reduce_scatter | solution.py:230
  647.7 33.2 %copy-start.4 = (bf16[3072,768]{1,0:T(8,128)(2,1)S(1)}, bf16[3072,768]{1,0:T(8,128)(2,1)}, u32[]{:S(2)}) copy-start(bf16[3072,768]{1,0:T(8,128)(2,1)} %copy-done.3) | copy-start | bytes 14155780
  647.7 62.6 %slice-start = ((s8[4718592]{0:T(1024)(128)(4,1)}), s8[4194304]{0:T(1024)(128)(4,1)S(1)}, s32[]{:S(2)}) async-start(s8[4718592]{0:T(1024)(128)(4,1)} %bitcast.91), calls=%async_computation.23 | async-start | bytes 8388608
  680.4 29.9 %collective-permute-start.2 = (f32[768,4480]{1,0:T(8,128)}, f32[768,4480]{1,0:T(8,128)}, u32[]{:S(2)}, u32[]{:S(2)}) collective-permute-start(f32[768,4480]{1,0:T(8,128)} %fusion.54), channel_id=1, source_target_pairs={{0,1},{1,0},{2,3},{3,2},{4,5},{5,4},{6,7},{7,6}} | collective-permute-start | bytes 41287688 | tf_op jit(solution)/shard_map/ppermute | solution.py:320
  680.9 29.4 %slice-start.1 = ((s8[4718592]{0:T(1024)(128)(4,1)}), s8[524288]{0:T(1024)(128)(4,1)S(1)}, s32[]{:S(2)}) async-start(s8[4718592]{0:T(1024)(128)(4,1)} %bitcast.91), calls=%async_computation.24 | async-start | bytes 1048576
  710.3 30.8 %collective-permute-start.3 = (f32[768,4480]{1,0:T(8,128)}, f32[768,4480]{1,0:T(8,128)}, u32[]{:S(2)}, u32[]{:S(2)}) collective-permute-start(f32[768,4480]{1,0:T(8,128)} %fusion.55), channel_id=1, source_target_pairs={{0,1},{1,0},{2,3},{3,2},{4,5},{5,4},{6,7},{7,6}} | collective-permute-start | bytes 41287688 | tf_op jit(solution)/shard_map/ppermute | solution.py:321
  741.1 850.7 %reduce-scatter.17.cloned.1.call-start = ((), (), s32[]{:S(2)}) async-start(), calls=%async_computation.19 | async-start | bytes 17203200 | tf_op jit(solution)/shard_map/reduce_scatter | solution.py:230
  855.0 33.4 %copy-start.5 = (bf16[3072,768]{1,0:T(8,128)(2,1)S(1)}, bf16[3072,768]{1,0:T(8,128)(2,1)}, u32[]{:S(2)}) copy-start(bf16[3072,768]{1,0:T(8,128)(2,1)} %copy-done.3) | copy-start | bytes 14155780
  887.8 31.5 %collective-permute-start.4 = (f32[768,4480]{1,0:T(8,128)}, f32[768,4480]{1,0:T(8,128)}, u32[]{:S(2)}, u32[]{:S(2)}) collective-permute-start(f32[768,4480]{1,0:T(8,128)} %fusion.56), channel_id=1, source_target_pairs={{0,1},{1,0},{2,3},{3,2},{4,5},{5,4},{6,7},{7,6}} | collective-permute-start | bytes 41287688 | tf_op jit(solution)/shard_map/ppermute | solution.py:320
  918.1 33.8 %collective-permute-start.5 = (f32[768,4480]{1,0:T(8,128)}, f32[768,4480]{1,0:T(8,128)}, u32[]{:S(2)}, u32[]{:S(2)}) collective-permute-start(f32[768,4480]{1,0:T(8,128)} %fusion.57), channel_id=1, source_target_pairs={{0,1},{1,0},{2,3},{3,2},{4,5},{5,4},{6,7},{7,6}} | collective-permute-start | bytes 41287688 | tf_op jit(solution)/shard_map/ppermute | solution.py:321
  919.3 675.4 %reduce-scatter.9.cloned.1.call-start = ((), (), s32[]{:S(2)}) async-start(), calls=%async_computation.15 | async-start | bytes 14155776 | tf_op jit(solution)/shard_map/reduce_scatter | solution.py:230
  1090.4 53.1 %copy-start.11 = (f32[1536]{0:T(1024)S(1)}, f32[1536]{0:T(1024)}, u32[]{:S(2)}) copy-start(f32[1536]{0:T(1024)} %copy-done.10) | copy-start | bytes 18436
  1090.4 53.1 %copy-start.12 = (f32[3072]{0:T(1024)S(1)}, f32[3072]{0:T(1024)}, u32[]{:S(2)}) copy-start(f32[3072]{0:T(1024)} %slice_reduce_fusion) | copy-start | bytes 36868
  1202.3 17.6 copy-start.7
  1216.1 3.7 copy-start.8
  1237.8 18.6 %copy-start.1 = (f32[3072,128]{1,0:T(8,128)S(1)}, f32[3072,128]{1,0:T(8,128)}, u32[]{:S(2)}) copy-start(f32[3072,128]{1,0:T(8,128)} %copy-done) | copy-start | bytes 4718596
  1256.4 106.7 %copy-start.15 = (f32[3072]{0:T(1024)S(1)}, f32[3072]{0:T(1024)}, u32[]{:S(2)}) copy-start(f32[3072]{0:T(1024)} %copy-done.14) | copy-start | bytes 36868
  1256.4 106.6 %copy-start.17 = (f32[1536]{0:T(1024)S(1)}, f32[1536]{0:T(1024)}, u32[]{:S(2)}) copy-start(f32[1536]{0:T(1024)} %copy-done.16) | copy-start | bytes 18436
  1390.7 214.6 %reduce-scatter.15.cloned.1.call-start = ((), (), s32[]{:S(2)}) async-start(), calls=%async_computation.18 | async-start | bytes 17203200 | tf_op jit(solution)/shard_map/reduce_scatter | solution.py:230
  1391.4 341.5 %reduce-scatter.19.cloned.1.call-start = ((), (), s32[]{:S(2)}) async-start(), calls=%async_computation.20 | async-start | bytes 17203200 | tf_op jit(solution)/shard_map/reduce_scatter | solution.py:230
  1392.0 413.2 %reduce-scatter.11.cloned.1.call-start = ((), (), s32[]{:S(2)}) async-start(), calls=%async_computation.16 | async-start | bytes 10616832 | tf_op jit(solution)/shard_map/reduce_scatter | solution.py:230
  1401.1 10.0 collective-permute-start.9
  1420.2 29.0 %slice-start.2 = ((s8[9437184]{0:T(1024)(128)(4,1)}), s8[1048576]{0:T(1024)(128)(4,1)S(1)}, s32[]{:S(2)}) async-start(s8[9437184]{0:T(1024)(128)(4,1)} %bitcast.98), calls=%async_computation.25 | async-start | bytes 2097152
  1420.2 28.4 %copy-start.13 = (f32[1536]{0:T(1024)S(1)}, f32[1536]{0:T(1024)}, u32[]{:S(2)}) copy-start(f32[1536]{0:T(1024)} %get-tuple-element.51) | copy-start | bytes 18436
  1420.2 29.0 %slice-start.3 = ((s8[9437184]{0:T(1024)(128)(4,1)}), s8[4194304]{0:T(1024)(128)(4,1)S(1)}, s32[]{:S(2)}) async-start(s8[9437184]{0:T(1024)(128)(4,1)} %bitcast.98), calls=%async_computation.26 | async-start | bytes 8388608
  1420.2 29.0 %slice-start.4 = ((s8[9437184]{0:T(1024)(128)(4,1)}), s8[4194304]{0:T(1024)(128)(4,1)S(1)}, s32[]{:S(2)}) async-start(s8[9437184]{0:T(1024)(128)(4,1)} %bitcast.98), calls=%async_computation.27 | async-start | bytes 8388608
  1448.7 24.4 %collective-permute-start.6 = (f32[26,128]{1,0:T(8,128)S(1)}, f32[26,128]{1,0:T(8,128)S(1)}, u32[]{:S(2)}, u32[]{:S(2)}) collective-permute-start(f32[26,128]{1,0:T(8,128)S(1)} %fusion.44), channel_id=1, source_target_pairs={{0,1},{1,0},{2,3},{3,2},{4,5},{5,4},{6,7},{7,6}} | collective-permute-start | bytes 39944 | tf_op jit(solution)/shard_map/ppermute | solution.py:233
  1473.1 56.3 %collective-permute-start.7 = (f32[26,128]{1,0:T(8,128)S(1)}, f32[26,128]{1,0:T(8,128)S(1)}, u32[]{:S(2)}, u32[]{:S(2)}) collective-permute-start(f32[26,128]{1,0:T(8,128)S(1)} %fusion.111), channel_id=1, source_target_pairs={{0,2},{2,0},{4,6},{6,4},{1,3},{3,1},{5,7},{7,5}} | collective-permute-start | bytes 39944 | tf_op jit(solution)/shard_map/ppermute | solution.py:236
  1529.4 56.0 %collective-permute-start.8 = (f32[26,128]{1,0:T(8,128)S(1)}, f32[26,128]{1,0:T(8,128)S(1)}, u32[]{:S(2)}, u32[]{:S(2)}) collective-permute-start(f32[26,128]{1,0:T(8,128)S(1)} %fusion.112), channel_id=1, source_target_pairs={{0,4},{2,6},{4,0},{6,2},{1,5},{3,7},{5,1},{7,3}} | collective-permute-start | bytes 39944 | tf_op jit(solution)/shard_map/ppermute | solution.py:236
Sparse Core Ops, SparseCore 0:
  18.9 44.2 all-gather.7
  65.0 33.2 all-gather.9
  100.1 71.4 all-gather.11
  173.3 71.4 all-gather.13
  246.4 71.4 all-gather.15
  319.5 71.4 all-gather.17
  392.8 131.4 all-gather.19
  527.3 124.6 reduce-scatter.20
  655.0 124.6 reduce-scatter.22
  782.6 124.6 reduce-scatter.12
  919.4 125.0 reduce-scatter.16
  1390.8 86.3 reduce-scatter.8
  1480.2 124.9 reduce-scatter.14
  1608.1 124.6 reduce-scatter.18
  1736.7 68.4 reduce-scatter.10
